TPU v7x, 32 devices: a whole 2x2x4 slice. The times are simulated.
32 devices in a mesh: parts: 2 (over x), blk: 16 (over z, y, core).
Axes of the slice: x: 2, y: 2, z: 4, core: 2. Of those that a mesh axis runs over, the one named last changes fastest.
Arguments:
- queries: bfloat16 [2048, 4096], P(('parts', 'blk')), parts along dimension 0, may hold values from -12 to 12
- keys: bfloat16 [2048, 512], P(('parts', 'blk')), parts along dimension 0, may hold values from -12 to 12
- values: bfloat16 [2048, 512], P(('parts', 'blk')), parts along dimension 0, may hold values from -6 to 6
- span_order: int32 [64], P('parts'), parts along dimension 0, may hold values from 0 to 31, as said below
Outputs:
- attended: bfloat16 [2048, 4096], P(('parts', 'blk')), parts along dimension 0
There are 2 independent parts, one for each index of `parts`. A program takes and returns all parts, laid end to end along the dimension named above; each array names one. Nothing has to cross between parts.
Inputs may be any that keep to these rules, and one draw needn't show every extreme that they name: `span_order`: a permutation of the 32 blocks; slots 2i and 2i+1 hold blocks c and 31 - c for some c.
All inputs are finite; a program needn't handle non-finite values.
Results may differ from a plain program's by a relative error of at most 0.0065.
Values may be sent and summed in bfloat16 or wider, within the bound.
No kernel may reach another device: no remote copies, remote signals or barrier semaphores. Data moves between devices by JAX's collectives and lax.ppermute only.
A program may use at most 64 MiB of HBM per device.

v0:
```python
import functools
import math

import jax
import jax.numpy as jnp
from jax import lax
from jax.experimental import pallas as pl
from jax.experimental.pallas import tpu as pltpu
from jax.sharding import PartitionSpec as P


HEAD = 128
CORES = 2
TILE_SPANS = 8
LANES = 128
SCALE = math.log2(math.e) / HEAD**0.5


def chip_at(place, chips):
    half = chips // 2
    return 2 * place if place < half else 2 * (chips - 1 - place) + 1


def place_of(chip, chips):
    return chip // 2 if chip % 2 == 0 else chips - 1 - chip // 2


def ring_pairs(size, sender, receiver, hops):
    chips = size // CORES
    pairs = []
    for device in range(size):
        chip, core = device // CORES, device % CORES
        ahead = core == sender
        place = (place_of(chip, chips) + (hops if ahead else -hops)) % chips
        target = receiver if ahead else 1 - receiver
        pairs.append((device, chip_at(place, chips) * CORES + target))
    return pairs


def mate_pairs(size):
    return [(device, device ^ 1) for device in range(size)]


def gather(mine):
    size = lax.axis_size("blk")
    far = size // CORES // 2

    def swap(array):
        return lax.ppermute(array, "blk", mate_pairs(size))

    def send(array, sender, receiver, hops):
        return lax.ppermute(array, "blk", ring_pairs(size, sender, receiver, hops))

    mate = swap(mine)
    pieces = [(mine, 0, 0, 0, True), (mate, 0, 0, 0, False)]
    lead = follow = None
    held = 0
    for step in range(1, far + 1):
        for rest in range(2 if step < far else 1):
            source = (mate if rest else mine) if step == 1 else (follow if rest else lead)
            got = send(source, held, 1 - held, 1)
            if rest:
                follow = got
            else:
                lead = got
            pieces.append((got, step, 1 - held, rest, True))
            pieces.append((swap(got), step, 1 - held, rest, False))
        held = 1 - held
    return pieces


def ring_spot(size):
    chips = size // CORES
    mine = lax.axis_index("blk")
    chip = mine // CORES
    place = jnp.where(chip % 2 == 0, chip // 2, chips - 1 - chip // 2)
    return mine, chip, mine % CORES, place, chips


def device_of(entry):
    distance, behind, rest, own = entry
    _, chip, core, place, chips = ring_spot(lax.axis_size("blk"))
    half = chips // 2
    holder = core if own else 1 - core
    if distance == 0:
        return chip * CORES + holder
    from_behind = (holder == behind).astype(jnp.int32)
    spot = (place + chips + distance - 2 * distance * from_behind) % chips
    from_chip = jnp.where(spot < half, 2 * spot, 2 * (chips - 1 - spot) + 1)
    return from_chip * CORES + rest + (1 - 2 * rest) * (1 - from_behind)


def blocks_of(piece, table):
    return [table[at // LANES, at % LANES] for at in (2 * piece, 2 * piece + 1)]


def own_blocks(table):
    first, second = blocks_of(0, table)
    in_order = first < second
    return in_order, jnp.minimum(first, second), jnp.maximum(first, second)


def setup_kernel(plan, order_ref, table):
    rows = table.shape[0]
    at = lax.broadcasted_iota(jnp.int32, (rows, LANES), 0) * LANES + lax.broadcasted_iota(
        jnp.int32, (rows, LANES), 1
    )
    wanted = jnp.zeros((rows, LANES), jnp.int32)
    for number, entry in enumerate(plan):
        device = device_of(entry)
        for slot in range(2):
            wanted = jnp.where(at == 2 * number + slot, device * 2 + slot, wanted)
    known = jnp.zeros((rows, LANES), jnp.int32)
    for block in range(order_ref.shape[1]):
        known = jnp.where(wanted == block, order_ref[0, block], known)
    table[...] = known


def load_kernel(table, q_ref, q_out, table_out):
    q_out[...] = q_ref[...]
    table_out[...] = table[...]


def place_kernel(numbers, missing, span, table, *refs):
    held = refs[-1]
    for number in missing:
        for block in blocks_of(number, table):
            at = pl.ds(pl.multiple_of(block * span, span), span)
            held[:, at, :] = jnp.zeros((held.shape[0], span, HEAD), held.dtype)
    for number, ref in zip(numbers, refs):
        for slot, block in enumerate(blocks_of(number, table)):
            at = pl.ds(pl.multiple_of(block * span, span), span)
            for part in range(held.shape[0]):
                held[part, at, :] = ref[
                    slot * span : (slot + 1) * span, part * HEAD : (part + 1) * HEAD
                ]


def place_first(numbers, missing, span, table, *refs):
    place_kernel(numbers, missing, span, table, *refs)


def place_aliased(numbers, missing, span, table, held_in, *refs):
    del held_in, missing
    place_kernel(numbers, [], span, table, *refs)


def head_columns(kv_head, g, group):
    return slice((kv_head * group + g) * HEAD, (kv_head * group + g + 1) * HEAD)


def query_rows(q_ref, span, kv_head, group, in_order):
    slots = [
        jnp.concatenate(
            [
                q_ref[slot * span : (slot + 1) * span, head_columns(kv_head, g, group)]
                for g in range(group)
            ],
            axis=0,
        )
        for slot in range(2)
    ]
    return jnp.where(in_order, slots[0], slots[1]), jnp.where(in_order, slots[1], slots[0])


def folded(array):
    parts = [array[:, at : at + HEAD] for at in range(0, array.shape[1], HEAD)]
    return functools.reduce(jnp.add, parts)


def attend_kernel(missing, kv_list, span, group, q_ref, table, held, sum_ref, top_ref, total_ref):
    kv_heads = held.shape[0] // 2
    tile = TILE_SPANS * span
    tiles = held.shape[1] // tile
    middle = tiles // 2
    in_order, low_pos, high_pos = own_blocks(table)
    absent = [block for number in missing for block in blocks_of(number, table)]
    gap = lax.broadcasted_iota(jnp.int32, (span, tile), 1) - lax.broadcasted_iota(
        jnp.int32, (span, tile), 0
    )
    lane_block = lax.broadcasted_iota(jnp.int32, (8, tile), 1) // span
    reach = low_pos // TILE_SPANS

    def bias_of(key_tile):
        block = lane_block + key_tile * TILE_SPANS
        gone = functools.reduce(jnp.logical_or, [block == b for b in absent])
        return jnp.where(gone, -jnp.inf, 0.0)

    def tile_of(part, key_tile):
        return held[part, key_tile * tile : (key_tile + 1) * tile, :]

    def scores(query, keys, key_tile, bias, limit):
        raw = lax.dot_general(
            query, keys, (((1,), (1,)), ((), ())), preferred_element_type=jnp.float32
        )
        raw = (raw.reshape(-1, 8, tile) + bias[None]).reshape(raw.shape)
        if limit is None:
            return raw
        keep = gap <= limit * span - key_tile * tile
        return jnp.where(keep[None], raw.reshape(-1, span, tile), -jnp.inf).reshape(raw.shape)

    def weighted(expo, rows_v):
        return jnp.dot(expo.astype(jnp.bfloat16), rows_v, preferred_element_type=jnp.float32)

    def top(items):
        return jnp.max(functools.reduce(jnp.maximum, items), axis=-1, keepdims=True)

    def expo_of(s, m):
        return jnp.exp2((s - m) * SCALE)

    extras = []
    for j in range(1, middle):
        is_low = reach >= j
        key_tile = jnp.where(is_low, j, tiles - j)
        limit = jnp.where(is_low, low_pos, high_pos)
        extras.append((j, is_low, key_tile, limit, bias_of(key_tile)))
    biases = [bias_of(t) for t in range(middle + 1)]
    for at, kv_head in enumerate(kv_list):
        low_q, high_q = query_rows(q_ref, span, kv_head, group, in_order)
        high_s = [
            scores(
                high_q, tile_of(kv_head, t), t, biases[t], high_pos if t == middle else None
            )
            for t in range(middle + 1)
        ]
        low_s = scores(low_q, tile_of(kv_head, 0), 0, biases[0], low_pos)
        high_m = top(high_s)
        low_m = top([low_s])
        extra_s = []
        for j, is_low, key_tile, limit, bias in extras:
            keys = jnp.where(is_low, tile_of(kv_head, j), tile_of(kv_head, tiles - j))
            s = scores(jnp.where(is_low, low_q, high_q), keys, key_tile, bias, limit)
            m = top([s])
            low_m = jnp.where(is_low, jnp.maximum(low_m, m), low_m)
            high_m = jnp.where(is_low, high_m, jnp.maximum(high_m, m))
            extra_s.append(s)
        high_l, high_o = 0.0, 0.0
        for t, s in enumerate(high_s):
            e = expo_of(s, high_m)
            high_l = high_l + folded(e)
            high_o = high_o + weighted(e, tile_of(kv_heads + kv_head, t))
        e = expo_of(low_s, low_m)
        low_l = folded(e)
        low_o = weighted(e, tile_of(kv_heads + kv_head, 0))
        for (j, is_low, key_tile, limit, bias), s in zip(extras, extra_s):
            e = expo_of(s, jnp.where(is_low, low_m, high_m))
            l = folded(e)
            v_part = kv_heads + kv_head
            o = weighted(e, jnp.where(is_low, tile_of(v_part, j), tile_of(v_part, tiles - j)))
            low_l = low_l + jnp.where(is_low, l, 0.0)
            high_l = high_l + jnp.where(is_low, 0.0, l)
            low_o = low_o + jnp.where(is_low, o, 0.0)
            high_o = high_o + jnp.where(is_low, 0.0, o)
        for side, (o, m, l) in enumerate(((low_o, low_m, low_l), (high_o, high_m, high_l))):
            sum_ref[at, side] = o
            top_ref[at, side] = jnp.broadcast_to(m, o.shape)
            total_ref[at, side] = l


def finish_kernel(plan, stages, span, group, kv_heads, q_ref, table, *refs):
    pieces = refs[: len(plan)]
    states = refs[len(plan) : len(plan) + 3 * len(stages)]
    out_ref, ready, sems = refs[len(plan) + 3 * len(stages) :]
    in_order, *positions = own_blocks(table)
    blocks = [block for number in plan for block in blocks_of(number, table)]
    keys = span * len(blocks)
    lane_block = lax.broadcasted_iota(jnp.int32, (8, keys), 1) // span
    position = functools.reduce(
        lambda held, item: jnp.where(lane_block == item[0], item[1], held),
        enumerate(blocks),
        jnp.zeros((8, keys), jnp.int32),
    )
    biases = [jnp.where(position < pos, 0.0, -jnp.inf) for pos in positions]
    width = kv_heads * HEAD

    def rows_of(column):
        return jnp.concatenate([ref[:, column : column + HEAD] for ref in pieces], axis=0)

    where = [(stage, at) for stage, kv_list in enumerate(stages) for at in range(len(kv_list))]
    tops, weights = [], []
    for kv_head, (stage, at) in enumerate(where):
        queries = query_rows(q_ref, span, kv_head, group, in_order)
        rows_k = rows_of(kv_head * HEAD)
        for side in range(2):
            s = lax.dot_general(
                queries[side], rows_k, (((1,), (1,)), ((), ())), preferred_element_type=jnp.float32
            )
            s = (s.reshape(-1, 8, keys) + biases[side][None]).reshape(s.shape)
            new_m = jnp.maximum(
                states[3 * stage + 1][at, side], jnp.max(s, axis=-1, keepdims=True)
            )
            tops.append(new_m)
            weights.append(jnp.exp2((s - new_m) * SCALE))
    copies = []
    for kv_head, (stage, at) in enumerate(where):
        rows_v = rows_of(width + kv_head * HEAD)
        normed = []
        for side in range(2):
            sum_ref, top_ref, total_ref = states[3 * stage : 3 * stage + 3]
            new_m, e = tops[2 * kv_head + side], weights[2 * kv_head + side]
            fade = jnp.exp2((top_ref[at, side] - new_m) * SCALE)
            l = jnp.sum(total_ref[at, side] * fade + folded(e), axis=-1, keepdims=True)
            o = sum_ref[at, side] * fade + jnp.dot(
                e.astype(jnp.bfloat16), rows_v, preferred_element_type=jnp.float32
            )
            normed.append((o / l).astype(jnp.bfloat16))
        low, high = normed
        for slot, rows in enumerate(
            (jnp.where(in_order, low, high), jnp.where(in_order, high, low))
        ):
            for g in range(group):
                ready[slot * span : (slot + 1) * span, head_columns(kv_head, g, group)] = rows[
                    g * span : (g + 1) * span
                ]
        columns = pl.ds(kv_head * group * HEAD, group * HEAD)
        copy = pltpu.make_async_copy(ready.at[:, columns], out_ref.at[:, columns], sems.at[kv_head])
        copy.start()
        copies.append(copy)
    for copy in copies:
        copy.wait()


def attended(queries, keys, values, span_order):
    rows = queries.shape[0]
    span = rows // 2
    kv_heads = keys.shape[1] // HEAD
    group = queries.shape[1] // (kv_heads * HEAD)
    size = lax.axis_size("blk")
    far = size // CORES // 2
    count = rows * size
    vmem = pl.BlockSpec(memory_space=pltpu.VMEM)
    anywhere = pl.BlockSpec(memory_space=pltpu.HBM)
    params = pltpu.CompilerParams(vmem_limit_bytes=8 * 2**20 + 6 * count * 2 * kv_heads * HEAD)

    def call(kernel, out_shape, in_specs, **extra):
        return pl.pallas_call(
            kernel, out_shape=out_shape, in_specs=in_specs, compiler_params=params, **extra
        )

    width = keys.shape[1]
    lowest = jnp.array(-jnp.inf, keys.dtype)
    mine = jnp.maximum(
        lax.pad(keys, lowest, ((0, 0, 0), (0, width, 0))),
        lax.pad(values, lowest, ((0, 0, 0), (width, 0, 0))),
    )
    pieces = gather(mine)
    plan = [p[1:] for p in pieces]
    table_rows = -(-2 * len(plan) // LANES)
    table = call(
        functools.partial(setup_kernel, plan),
        jax.ShapeDtypeStruct((table_rows, LANES), jnp.int32),
        [vmem],
        out_specs=vmem,
    )(span_order.reshape(1, -1))
    q_held, loaded = call(
        load_kernel,
        (
            jax.ShapeDtypeStruct(queries.shape, queries.dtype),
            jax.ShapeDtypeStruct(table.shape, table.dtype),
        ),
        [vmem, vmem],
        out_specs=(vmem, vmem),
    )(table, queries)
    missing = [number for number, entry in enumerate(plan) if entry[0] == far]
    last = [pieces[number] for number in missing]
    held_shape = jax.ShapeDtypeStruct((2 * kv_heads, count, HEAD), jnp.bfloat16)
    held = None
    placed = set(missing)
    for step in range(2, far + 1):
        numbers = []
        for number, entry in enumerate(plan):
            ready = step == far or entry[0] < step - 1 or (entry[0] == step - 1 and entry[3])
            if ready and number not in placed:
                numbers.append(number)
        placed.update(numbers)
        held = call(
            functools.partial(place_first if held is None else place_aliased, numbers, missing, span),
            held_shape,
            [vmem] * (len(numbers) + 1 + (held is not None)),
            out_specs=vmem,
            **({} if held is None else {"input_output_aliases": {1: 0}}),
        )(
            loaded if step == far else table,
            *([] if held is None else [held]),
            *[pieces[n][0] for n in numbers],
        )
    stages = [list(range(kv_heads // 2)), list(range(kv_heads // 2, kv_heads))]
    states = []
    for kv_list in stages:
        shape = jax.ShapeDtypeStruct((len(kv_list), 2, group * span, HEAD), jnp.float32)
        states += call(
            functools.partial(attend_kernel, missing, kv_list, span, group),
            (shape, shape, shape),
            [vmem, vmem, vmem],
            out_specs=(vmem, vmem, vmem),
        )(q_held, table, held)
    return call(
        functools.partial(finish_kernel, missing, stages, span, group, kv_heads),
        jax.ShapeDtypeStruct(queries.shape, jnp.bfloat16),
        [vmem] * (2 + len(last) + len(states)),
        out_specs=anywhere,
        scratch_shapes=[
            pltpu.VMEM(queries.shape, jnp.bfloat16),
            pltpu.SemaphoreType.DMA((kv_heads,)),
        ],
    )(q_held, table, *[p[0] for p in last], *states)


def solution(mesh):
    return jax.shard_map(
        attended,
        mesh=mesh,
        in_specs=(
            P(("parts", "blk"), None),
            P(("parts", "blk"), None),
            P(("parts", "blk"), None),
            P("parts"),
        ),
        out_specs=P(("parts", "blk"), None),
        check_vma=False,
    )
```

profile of v0, /device:TPU:0, one launch (start us, length us, event | category | flops | bytes accessed | tf_op | source)
XLA Modules:
  0.0 28.6 jit_solution(7121319334037274949)
XLA Ops:
  0.0 0.9 %pad_maximum_fusion.refs_0_ = bf16[64,1024]{1,0:T(8,128)(2,1)S(1)} fusion(bf16[64,512]{1,0:T(8,128)(2,1)} %param.6, bf16[64,512]{1,0:T(8,128)(2,1)} %param.5), kind=kLoop, calls=%fused_computation | loop fusion | flops 262144 | bytes 262144 | tf_op jit(solution)/shard_map/max | solution.py:342
  0.9 0.6 %collective-permute-start.5 = (bf16[64,1024]{1,0:T(8,128)(2,1)S(1)}, bf16[64,1024]{1,0:T(8,128)(2,1)S(1)}, u32[]{:S(2)}, u32[]{:S(2)}) collective-permute-start(bf16[64,1024]{1,0:T(8,128)(2,1)S(1)} %pad_maximum_fusion.refs_0_), channel_id=1, source_target_pairs={{0,1},{1,0},{2,3},{3,2},{4,5},{5,4},{6,7},{7,6},{8,9},{9,8},{10,11... | collective-permute-start | bytes 393224 | tf_op jit(solution)/shard_map/ppermute | solution.py:49
  1.4 2.7 %collective-permute-start = (bf16[64,1024]{1,0:T(8,128)(2,1)S(1)}, bf16[64,1024]{1,0:T(8,128)(2,1)S(1)}, u32[]{:S(2)}, u32[]{:S(2)}) collective-permute-start(bf16[64,1024]{1,0:T(8,128)(2,1)S(1)} %pad_maximum_fusion.refs_0_), channel_id=1, source_target_pairs={{0,5},{1,2},{2,1},{3,6},{4,9},{5,0},{6,3},{7,10},{8,13},{9,4},{10,... | collective-permute-start | bytes 393224 | tf_op jit(solution)/shard_map/ppermute | solution.py:52
  4.1 1.0 %collective-permute-start.6 = (bf16[64,1024]{1,0:T(8,128)(2,1)S(1)}, bf16[64,1024]{1,0:T(8,128)(2,1)S(1)}, u32[]{:S(2)}, u32[]{:S(2)}) collective-permute-start(bf16[64,1024]{1,0:T(8,128)(2,1)S(1)} %collective-permute-done.5.refs_1_), channel_id=1, source_target_pairs={{0,5},{1,2},{2,1},{3,6},{4,9},{5,0},{6,3},{7,10},{8,13},{9,4},{10,... | collective-permute-start | bytes 393224 | tf_op jit(solution)/shard_map/ppermute | solution.py:52
  5.1 1.7 %collective-permute-done.refs_2_ = bf16[64,1024]{1,0:T(8,128)(2,1)S(1)} collective-permute-done((bf16[64,1024]{1,0:T(8,128)(2,1)S(1)}, bf16[64,1024]{1,0:T(8,128)(2,1)S(1)}, u32[]{:S(2)}, u32[]{:S(2)}) %collective-permute-start) | collective-permute-done | bytes 131104 | tf_op jit(solution)/shard_map/ppermute | solution.py:52
  6.8 2.0 %collective-permute-start.1 = (bf16[64,1024]{1,0:T(8,128)(2,1)S(1)}, bf16[64,1024]{1,0:T(8,128)(2,1)S(1)}, u32[]{:S(2)}, u32[]{:S(2)}) collective-permute-start(bf16[64,1024]{1,0:T(8,128)(2,1)S(1)} %collective-permute-done.refs_2_), channel_id=1, source_target_pairs={{0,3},{1,4},{2,7},{3,0},{4,1},{5,8},{6,11},{7,2},{8,5},{9,12},{10,... | collective-permute-start | bytes 393224 | tf_op jit(solution)/shard_map/ppermute | solution.py:52
  8.8 1.1 %collective-permute-start.9 = (bf16[64,1024]{1,0:T(8,128)(2,1)S(1)}, bf16[64,1024]{1,0:T(8,128)(2,1)S(1)}, u32[]{:S(2)}, u32[]{:S(2)}) collective-permute-start(bf16[64,1024]{1,0:T(8,128)(2,1)S(1)} %collective-permute-done.6.refs_3_), channel_id=1, source_target_pairs={{0,3},{1,4},{2,7},{3,0},{4,1},{5,8},{6,11},{7,2},{8,5},{9,12},{10,... | collective-permute-start | bytes 393224 | tf_op jit(solution)/shard_map/ppermute | solution.py:52
  9.9 1.5 %collective-permute-done.1.refs_2_ = bf16[64,1024]{1,0:T(8,128)(2,1)S(1)} collective-permute-done((bf16[64,1024]{1,0:T(8,128)(2,1)S(1)}, bf16[64,1024]{1,0:T(8,128)(2,1)S(1)}, u32[]{:S(2)}, u32[]{:S(2)}) %collective-permute-start.1) | collective-permute-done | bytes 131104 | tf_op jit(solution)/shard_map/ppermute | solution.py:52
  11.4 2.1 %collective-permute-start.2 = (bf16[64,1024]{1,0:T(8,128)(2,1)S(1)}, bf16[64,1024]{1,0:T(8,128)(2,1)S(1)}, u32[]{:S(2)}, u32[]{:S(2)}) collective-permute-start(bf16[64,1024]{1,0:T(8,128)(2,1)S(1)} %collective-permute-done.1.refs_2_), channel_id=1, source_target_pairs={{0,5},{1,2},{2,1},{3,6},{4,9},{5,0},{6,3},{7,10},{8,13},{9,4},{10,... | collective-permute-start | bytes 393224 | tf_op jit(solution)/shard_map/ppermute | solution.py:52
  13.5 0.5 %collective-permute-start.8 = (bf16[64,1024]{1,0:T(8,128)(2,1)S(1)}, bf16[64,1024]{1,0:T(8,128)(2,1)S(1)}, u32[]{:S(2)}, u32[]{:S(2)}) collective-permute-start(bf16[64,1024]{1,0:T(8,128)(2,1)S(1)} %collective-permute-done.6.refs_3_), channel_id=1, source_target_pairs={{0,1},{1,0},{2,3},{3,2},{4,5},{5,4},{6,7},{7,6},{8,9},{9,8},{10,11... | collective-permute-start | bytes 393224 | tf_op jit(solution)/shard_map/ppermute | solution.py:49
  14.0 1.2 %collective-permute-start.13 = (bf16[64,1024]{1,0:T(8,128)(2,1)S(1)}, bf16[64,1024]{1,0:T(8,128)(2,1)S(1)}, u32[]{:S(2)}, u32[]{:S(2)}) collective-permute-start(bf16[64,1024]{1,0:T(8,128)(2,1)S(1)} %collective-permute-done.9.refs_3_), channel_id=1, source_target_pairs={{0,5},{1,2},{2,1},{3,6},{4,9},{5,0},{6,3},{7,10},{8,13},{9,4},{10,... | collective-permute-start | bytes 393224 | tf_op jit(solution)/shard_map/ppermute | solution.py:52
  15.2 1.0 %collective-permute-done.2.refs_2_ = bf16[64,1024]{1,0:T(8,128)(2,1)S(1)} collective-permute-done((bf16[64,1024]{1,0:T(8,128)(2,1)S(1)}, bf16[64,1024]{1,0:T(8,128)(2,1)S(1)}, u32[]{:S(2)}, u32[]{:S(2)}) %collective-permute-start.2) | collective-permute-done | bytes 131104 | tf_op jit(solution)/shard_map/ppermute | solution.py:52
  16.1 2.0 %collective-permute-start.3 = (bf16[64,1024]{1,0:T(8,128)(2,1)S(1)}, bf16[64,1024]{1,0:T(8,128)(2,1)S(1)}, u32[]{:S(2)}, u32[]{:S(2)}) collective-permute-start(bf16[64,1024]{1,0:T(8,128)(2,1)S(1)} %collective-permute-done.2.refs_2_), channel_id=1, source_target_pairs={{0,3},{1,4},{2,7},{3,0},{4,1},{5,8},{6,11},{7,2},{8,5},{9,12},{10,... | collective-permute-start | bytes 393224 | tf_op jit(solution)/shard_map/ppermute | solution.py:52
  18.1 0.5 %collective-permute-start.12 = (bf16[64,1024]{1,0:T(8,128)(2,1)S(1)}, bf16[64,1024]{1,0:T(8,128)(2,1)S(1)}, u32[]{:S(2)}, u32[]{:S(2)}) collective-permute-start(bf16[64,1024]{1,0:T(8,128)(2,1)S(1)} %collective-permute-done.2.refs_2_), channel_id=1, source_target_pairs={{0,1},{1,0},{2,3},{3,2},{4,5},{5,4},{6,7},{7,6},{8,9},{9,8},{10,11... | collective-permute-start | bytes 393224 | tf_op jit(solution)/shard_map/ppermute | solution.py:49
  18.7 0.4 %collective-permute-start.14 = (bf16[64,1024]{1,0:T(8,128)(2,1)S(1)}, bf16[64,1024]{1,0:T(8,128)(2,1)S(1)}, u32[]{:S(2)}, u32[]{:S(2)}) collective-permute-start(bf16[64,1024]{1,0:T(8,128)(2,1)S(1)} %collective-permute-done.13.refs_4_), channel_id=1, source_target_pairs={{0,1},{1,0},{2,3},{3,2},{4,5},{5,4},{6,7},{7,6},{8,9},{9,8},{10,11... | collective-permute-start | bytes 393224 | tf_op jit(solution)/shard_map/ppermute | solution.py:49
  19.2 1.6 %collective-permute-done.3.refs_0_ = bf16[64,1024]{1,0:T(8,128)(2,1)S(1)} collective-permute-done((bf16[64,1024]{1,0:T(8,128)(2,1)S(1)}, bf16[64,1024]{1,0:T(8,128)(2,1)S(1)}, u32[]{:S(2)}, u32[]{:S(2)}) %collective-permute-start.3) | collective-permute-done | bytes 131104 | tf_op jit(solution)/shard_map/ppermute | solution.py:52
  20.9 0.7 %copy-done.1 = s32[32]{0:T(128)S(1)} copy-done((s32[32]{0:T(128)S(1)}, s32[32]{0:T(128)}, u32[]{:S(2)}) %copy-start.1) | copy-done | bytes 152
  21.7 1.0 %copy-done = bf16[64,4096]{1,0:T(8,128)(2,1)S(1)} copy-done((bf16[64,4096]{1,0:T(8,128)(2,1)S(1)}, bf16[64,4096]{1,0:T(8,128)(2,1)}, u32[]{:S(2)}) %copy-start) | copy-done | bytes 524312
  22.8 0.2 shard_map.48.held_in
  23.0 0.2 shard_map.49.held_in
  23.3 0.2 shard_map.50.held
  23.5 1.6 %shard_map.52 = (f32[2,2,256,128]{3,2,1,0:T(8,128)S(1)}, f32[2,2,256,128]{3,2,1,0:T(8,128)S(1)}, f32[2,2,256,128]{3,2,1,0:T(8,128)S(1)}) custom-call(bf16[64,4096]{1,0:T(8,128)(2,1)S(1)} %get-tuple-element.13.q_ref, s32[1,128]{1,0:T(1,128)S(1)} %shard_map.46.table, bf16[8,1024,128]{2,1,0:T(8,128)(2,1)S(1)} %shard_map.50.held), custom_call_target="tpu_custom_call" | custom-call | tf_op jit(solution)/shard_map/pallas_call | solution.py:391
  25.1 1.6 %shard_map.51 = (f32[2,2,256,128]{3,2,1,0:T(8,128)S(1)}, f32[2,2,256,128]{3,2,1,0:T(8,128)S(1)}, f32[2,2,256,128]{3,2,1,0:T(8,128)S(1)}) custom-call(bf16[64,4096]{1,0:T(8,128)(2,1)S(1)} %get-tuple-element.13.q_ref, s32[1,128]{1,0:T(1,128)S(1)} %shard_map.46.table, bf16[8,1024,128]{2,1,0:T(8,128)(2,1)S(1)} %shard_map.50.held), custom_call_target="tpu_custom_call" | custom-call | tf_op jit(solution)/shard_map/pallas_call | solution.py:391
  26.7 1.8 %shard_map.53 = bf16[64,4096]{1,0:T(8,128)(2,1)} custom-call(bf16[64,4096]{1,0:T(8,128)(2,1)S(1)} %get-tuple-element.13.q_ref, s32[1,128]{1,0:T(1,128)S(1)} %shard_map.46.table, bf16[64,1024]{1,0:T(8,128)(2,1)S(1)} %collective-permute-done.3.refs_0_, bf16[64,1024]{1,0:T(8,128)(2,1)S(1)} %collective-permute-done.4.refs_1_, ...), custom_call_target="tpu_custom_call" | custom-call | tf_op jit(solution)/shard_map/pallas_call | solution.py:397
  (19 shorter events, 0.4 us)
Async XLA Ops:
  0.9 3.2 %collective-permute-start.5 = (bf16[64,1024]{1,0:T(8,128)(2,1)S(1)}, bf16[64,1024]{1,0:T(8,128)(2,1)S(1)}, u32[]{:S(2)}, u32[]{:S(2)}) collective-permute-start(bf16[64,1024]{1,0:T(8,128)(2,1)S(1)} %pad_maximum_fusion.refs_0_), channel_id=1, source_target_pairs={{0,1},{1,0},{2,3},{3,2},{4,5},{5,4},{6,7},{7,6},{8,9},{9,8},{10,11... | collective-permute-start | bytes 393224 | tf_op jit(solution)/shard_map/ppermute | solution.py:49
  1.4 5.3 %collective-permute-start = (bf16[64,1024]{1,0:T(8,128)(2,1)S(1)}, bf16[64,1024]{1,0:T(8,128)(2,1)S(1)}, u32[]{:S(2)}, u32[]{:S(2)}) collective-permute-start(bf16[64,1024]{1,0:T(8,128)(2,1)S(1)} %pad_maximum_fusion.refs_0_), channel_id=1, source_target_pairs={{0,5},{1,2},{2,1},{3,6},{4,9},{5,0},{6,3},{7,10},{8,13},{9,4},{10,... | collective-permute-start | bytes 393224 | tf_op jit(solution)/shard_map/ppermute | solution.py:52
  4.1 4.6 %collective-permute-start.6 = (bf16[64,1024]{1,0:T(8,128)(2,1)S(1)}, bf16[64,1024]{1,0:T(8,128)(2,1)S(1)}, u32[]{:S(2)}, u32[]{:S(2)}) collective-permute-start(bf16[64,1024]{1,0:T(8,128)(2,1)S(1)} %collective-permute-done.5.refs_1_), channel_id=1, source_target_pairs={{0,5},{1,2},{2,1},{3,6},{4,9},{5,0},{6,3},{7,10},{8,13},{9,4},{10,... | collective-permute-start | bytes 393224 | tf_op jit(solution)/shard_map/ppermute | solution.py:52
  6.8 4.6 %collective-permute-start.1 = (bf16[64,1024]{1,0:T(8,128)(2,1)S(1)}, bf16[64,1024]{1,0:T(8,128)(2,1)S(1)}, u32[]{:S(2)}, u32[]{:S(2)}) collective-permute-start(bf16[64,1024]{1,0:T(8,128)(2,1)S(1)} %collective-permute-done.refs_2_), channel_id=1, source_target_pairs={{0,3},{1,4},{2,7},{3,0},{4,1},{5,8},{6,11},{7,2},{8,5},{9,12},{10,... | collective-permute-start | bytes 393224 | tf_op jit(solution)/shard_map/ppermute | solution.py:52
  8.8 5.3 %collective-permute-start.9 = (bf16[64,1024]{1,0:T(8,128)(2,1)S(1)}, bf16[64,1024]{1,0:T(8,128)(2,1)S(1)}, u32[]{:S(2)}, u32[]{:S(2)}) collective-permute-start(bf16[64,1024]{1,0:T(8,128)(2,1)S(1)} %collective-permute-done.6.refs_3_), channel_id=1, source_target_pairs={{0,3},{1,4},{2,7},{3,0},{4,1},{5,8},{6,11},{7,2},{8,5},{9,12},{10,... | collective-permute-start | bytes 393224 | tf_op jit(solution)/shard_map/ppermute | solution.py:52
  11.4 4.7 %collective-permute-start.2 = (bf16[64,1024]{1,0:T(8,128)(2,1)S(1)}, bf16[64,1024]{1,0:T(8,128)(2,1)S(1)}, u32[]{:S(2)}, u32[]{:S(2)}) collective-permute-start(bf16[64,1024]{1,0:T(8,128)(2,1)S(1)} %collective-permute-done.1.refs_2_), channel_id=1, source_target_pairs={{0,5},{1,2},{2,1},{3,6},{4,9},{5,0},{6,3},{7,10},{8,13},{9,4},{10,... | collective-permute-start | bytes 393224 | tf_op jit(solution)/shard_map/ppermute | solution.py:52
  13.5 4.6 %collective-permute-start.7 = (bf16[64,1024]{1,0:T(8,128)(2,1)S(1)}, bf16[64,1024]{1,0:T(8,128)(2,1)S(1)}, u32[]{:S(2)}, u32[]{:S(2)}) collective-permute-start(bf16[64,1024]{1,0:T(8,128)(2,1)S(1)} %collective-permute-done.refs_2_), channel_id=1, source_target_pairs={{0,1},{1,0},{2,3},{3,2},{4,5},{5,4},{6,7},{7,6},{8,9},{9,8},{10,11... | collective-permute-start | bytes 393224 | tf_op jit(solution)/shard_map/ppermute | solution.py:49
  13.5 5.1 %collective-permute-start.8 = (bf16[64,1024]{1,0:T(8,128)(2,1)S(1)}, bf16[64,1024]{1,0:T(8,128)(2,1)S(1)}, u32[]{:S(2)}, u32[]{:S(2)}) collective-permute-start(bf16[64,1024]{1,0:T(8,128)(2,1)S(1)} %collective-permute-done.6.refs_3_), channel_id=1, source_target_pairs={{0,1},{1,0},{2,3},{3,2},{4,5},{5,4},{6,7},{7,6},{8,9},{9,8},{10,11... | collective-permute-start | bytes 393224 | tf_op jit(solution)/shard_map/ppermute | solution.py:49
  14.0 4.7 %collective-permute-start.13 = (bf16[64,1024]{1,0:T(8,128)(2,1)S(1)}, bf16[64,1024]{1,0:T(8,128)(2,1)S(1)}, u32[]{:S(2)}, u32[]{:S(2)}) collective-permute-start(bf16[64,1024]{1,0:T(8,128)(2,1)S(1)} %collective-permute-done.9.refs_3_), channel_id=1, source_target_pairs={{0,5},{1,2},{2,1},{3,6},{4,9},{5,0},{6,3},{7,10},{8,13},{9,4},{10,... | collective-permute-start | bytes 393224 | tf_op jit(solution)/shard_map/ppermute | solution.py:52
  16.1 4.6 %collective-permute-start.3 = (bf16[64,1024]{1,0:T(8,128)(2,1)S(1)}, bf16[64,1024]{1,0:T(8,128)(2,1)S(1)}, u32[]{:S(2)}, u32[]{:S(2)}) collective-permute-start(bf16[64,1024]{1,0:T(8,128)(2,1)S(1)} %collective-permute-done.2.refs_2_), channel_id=1, source_target_pairs={{0,3},{1,4},{2,7},{3,0},{4,1},{5,8},{6,11},{7,2},{8,5},{9,12},{10,... | collective-permute-start | bytes 393224 | tf_op jit(solution)/shard_map/ppermute | solution.py:52
  18.1 5.1 %collective-permute-start.10 = (bf16[64,1024]{1,0:T(8,128)(2,1)S(1)}, bf16[64,1024]{1,0:T(8,128)(2,1)S(1)}, u32[]{:S(2)}, u32[]{:S(2)}) collective-permute-start(bf16[64,1024]{1,0:T(8,128)(2,1)S(1)} %collective-permute-done.1.refs_2_), channel_id=1, source_target_pairs={{0,1},{1,0},{2,3},{3,2},{4,5},{5,4},{6,7},{7,6},{8,9},{9,8},{10,11... | collective-permute-start | bytes 393224 | tf_op jit(solution)/shard_map/ppermute | solution.py:49
  18.1 5.1 %collective-permute-start.12 = (bf16[64,1024]{1,0:T(8,128)(2,1)S(1)}, bf16[64,1024]{1,0:T(8,128)(2,1)S(1)}, u32[]{:S(2)}, u32[]{:S(2)}) collective-permute-start(bf16[64,1024]{1,0:T(8,128)(2,1)S(1)} %collective-permute-done.2.refs_2_), channel_id=1, source_target_pairs={{0,1},{1,0},{2,3},{3,2},{4,5},{5,4},{6,7},{7,6},{8,9},{9,8},{10,11... | collective-permute-start | bytes 393224 | tf_op jit(solution)/shard_map/ppermute | solution.py:49
  18.6 4.6 %collective-permute-start.11 = (bf16[64,1024]{1,0:T(8,128)(2,1)S(1)}, bf16[64,1024]{1,0:T(8,128)(2,1)S(1)}, u32[]{:S(2)}, u32[]{:S(2)}) collective-permute-start(bf16[64,1024]{1,0:T(8,128)(2,1)S(1)} %collective-permute-done.9.refs_3_), channel_id=1, source_target_pairs={{0,1},{1,0},{2,3},{3,2},{4,5},{5,4},{6,7},{7,6},{8,9},{9,8},{10,11... | collective-permute-start | bytes 393224 | tf_op jit(solution)/shard_map/ppermute | solution.py:49
  18.7 4.5 %collective-permute-start.14 = (bf16[64,1024]{1,0:T(8,128)(2,1)S(1)}, bf16[64,1024]{1,0:T(8,128)(2,1)S(1)}, u32[]{:S(2)}, u32[]{:S(2)}) collective-permute-start(bf16[64,1024]{1,0:T(8,128)(2,1)S(1)} %collective-permute-done.13.refs_4_), channel_id=1, source_target_pairs={{0,1},{1,0},{2,3},{3,2},{4,5},{5,4},{6,7},{7,6},{8,9},{9,8},{10,11... | collective-permute-start | bytes 393224 | tf_op jit(solution)/shard_map/ppermute | solution.py:49
  20.8 6.0 %collective-permute-start.4 = (bf16[64,1024]{1,0:T(8,128)(2,1)S(1)}, bf16[64,1024]{1,0:T(8,128)(2,1)S(1)}, u32[]{:S(2)}, u32[]{:S(2)}) collective-permute-start(bf16[64,1024]{1,0:T(8,128)(2,1)S(1)} %collective-permute-done.3.refs_0_), channel_id=1, source_target_pairs={{0,1},{1,0},{2,3},{3,2},{4,5},{5,4},{6,7},{7,6},{8,9},{9,8},{10,11... | collective-permute-start | bytes 393224 | tf_op jit(solution)/shard_map/ppermute | solution.py:49
  20.9 0.7 %copy-start.1 = (s32[32]{0:T(128)S(1)}, s32[32]{0:T(128)}, u32[]{:S(2)}) copy-start(s32[32]{0:T(128)} %param.7) | copy-start | bytes 388
  21.7 1.0 %copy-start = (bf16[64,4096]{1,0:T(8,128)(2,1)S(1)}, bf16[64,4096]{1,0:T(8,128)(2,1)}, u32[]{:S(2)}) copy-start(bf16[64,4096]{1,0:T(8,128)(2,1)} %q_ref.1) | copy-start | bytes 1572868
where the time goes:
time: 28.8 us; the launch traced here: 28.6 us
  starting transfers between devices  14.2 us (49%)
  Pallas kernels  5.89 us (20%)
  waiting for transfers between devices  5.8 us (20%)
  local copies, waits for them, and re-layouts  1.69 us (6%)
  other arithmetic  0.88 us (3%)
    ppermute x7, starting transfers between devices, send(): return lax.ppermute(array, 'blk', ring_pairs(size, sender, receiver, hops))  12 us
    ppermute x7, waiting for transfers between devices, send(): return lax.ppermute(array, 'blk', ring_pairs(size, sender, receiver, hops))  5.78 us
    pallas_call x2, Pallas kernels, attended(): call(functools.partial(attend_kernel, missing, kv_list, span, group), (sh...  3.2 us
    ppermute x8, starting transfers between devices, swap(): return lax.ppermute(array, 'blk', mate_pairs(size))  2.2 us
    pallas_call x1, Pallas kernels, attended(): call(functools.partial(finish_kernel, missing, stages, span, group, kv_he...  1.83 us
    unnamed x4, local copies, waits for them, and re-layouts  1.69 us
    max x1, other arithmetic, attended(): jnp.maximum(lax.pad(keys, lowest, ((0, 0, 0), (0, width, 0))), lax.pad(va...  0.88 us
    pallas_call x3, Pallas kernels, attended(): call(functools.partial(place_first if held is None else place_aliased, nu...  0.68 us
  transfers between devices with their start and end apart: 15, of which 4 were waited for; matrix products, arithmetic and copies ran while one was open for 0% of the time, Pallas kernels for 14%

commit v1 on v0

v1 whole, which is shorter than its diff:
```python
import functools
import math

import jax
import jax.numpy as jnp
from jax import lax
from jax.experimental import pallas as pl
from jax.experimental.pallas import tpu as pltpu
from jax.sharding import PartitionSpec as P


HEAD = 128
CORES = 2
TILE_SPANS = 8
LANES = 128
CUTS = 2
SCALE = math.log2(math.e) / HEAD**0.5


def chip_at(place, chips):
    half = chips // 2
    return 2 * place if place < half else 2 * (chips - 1 - place) + 1


def place_of(chip, chips):
    return chip // 2 if chip % 2 == 0 else chips - 1 - chip // 2


def ring_pairs(size, sender, receiver, hops):
    chips = size // CORES
    pairs = []
    for device in range(size):
        chip, core = device // CORES, device % CORES
        ahead = core == sender
        place = (place_of(chip, chips) + (hops if ahead else -hops)) % chips
        target = receiver if ahead else 1 - receiver
        pairs.append((device, chip_at(place, chips) * CORES + target))
    return pairs


def mate_pairs(size):
    return [(device, device ^ 1) for device in range(size)]


def gather(mine):
    size = lax.axis_size("blk")
    far = size // CORES // 2

    def swap(array):
        return lax.ppermute(array, "blk", mate_pairs(size))

    def send(array, sender, receiver, hops):
        return lax.ppermute(array, "blk", ring_pairs(size, sender, receiver, hops))

    mate = swap(mine)
    pieces = [(mine, 0, 0, 0, True), (mate, 0, 0, 0, False)]
    lead = follow = None
    held = 0
    for step in range(1, far + 1):
        for rest in range(2 if step < far else 1):
            source = (mate if rest else mine) if step == 1 else (follow if rest else lead)
            got = send(source, held, 1 - held, 1)
            if rest:
                follow = got
            else:
                lead = got
            pieces.append((got, step, 1 - held, rest, True))
            pieces.append((swap(got), step, 1 - held, rest, False))
        held = 1 - held
    return pieces


def ring_spot(size):
    chips = size // CORES
    mine = lax.axis_index("blk")
    chip = mine // CORES
    place = jnp.where(chip % 2 == 0, chip // 2, chips - 1 - chip // 2)
    return mine, chip, mine % CORES, place, chips


def device_of(entry):
    distance, behind, rest, own = entry
    _, chip, core, place, chips = ring_spot(lax.axis_size("blk"))
    half = chips // 2
    holder = core if own else 1 - core
    if distance == 0:
        return chip * CORES + holder
    from_behind = (holder == behind).astype(jnp.int32)
    spot = (place + chips + distance - 2 * distance * from_behind) % chips
    from_chip = jnp.where(spot < half, 2 * spot, 2 * (chips - 1 - spot) + 1)
    return from_chip * CORES + rest + (1 - 2 * rest) * (1 - from_behind)


def blocks_of(piece, table):
    return [table[at // LANES, at % LANES] for at in (2 * piece, 2 * piece + 1)]


def own_blocks(table):
    first, second = blocks_of(0, table)
    in_order = first < second
    return in_order, jnp.minimum(first, second), jnp.maximum(first, second)


def setup_kernel(plan, order_ref, table):
    rows = table.shape[0]
    at = lax.broadcasted_iota(jnp.int32, (rows, LANES), 0) * LANES + lax.broadcasted_iota(
        jnp.int32, (rows, LANES), 1
    )
    wanted = jnp.zeros((rows, LANES), jnp.int32)
    for number, entry in enumerate(plan):
        device = device_of(entry)
        for slot in range(2):
            wanted = jnp.where(at == 2 * number + slot, device * 2 + slot, wanted)
    known = jnp.zeros((rows, LANES), jnp.int32)
    for block in range(order_ref.shape[1]):
        known = jnp.where(wanted == block, order_ref[0, block], known)
    table[...] = known


def load_kernel(table, q_ref, q_out, table_out):
    q_out[...] = q_ref[...]
    table_out[...] = table[...]


def put_block(held, block, span, rows, present):
    at = pl.ds(pl.multiple_of(block * span, span), span)
    parts = held.shape[0] - 1
    for part in range(parts):
        held[part, at, :] = rows(part)
    held[parts, at, :] = jnp.full((span, HEAD), present, held.dtype)


def place_kernel(numbers, span, table, pieces, held):
    for number, ref in zip(numbers, pieces):
        for slot, block in enumerate(blocks_of(number, table)):
            put_block(
                held,
                block,
                span,
                lambda part: ref[slot * span : (slot + 1) * span, part * HEAD : (part + 1) * HEAD],
                1.0,
            )


def place_first(numbers, missing, span, table, *refs):
    *pieces, held = refs
    mine = pieces[0]
    in_order, _, _ = own_blocks(table)
    keys = (held.shape[0] - 1) // 2

    def stand_in(part):
        if part >= keys:
            return jnp.zeros((span, HEAD), held.dtype)
        columns = slice(part * HEAD, (part + 1) * HEAD)
        both = [mine[slot * span : slot * span + 1, columns].astype(jnp.float32) for slot in range(2)]
        row = jnp.where(in_order, both[0], both[1])
        return jnp.broadcast_to(row, (span, HEAD)).astype(held.dtype)

    fills = [stand_in(part) for part in range(2 * keys)]
    for number in missing:
        for block in blocks_of(number, table):
            put_block(held, block, span, lambda part: fills[part], 0.0)
    place_kernel(numbers, span, table, pieces, held)


def place_more(numbers, span, table, held_in, *refs):
    del held_in
    *pieces, held = refs
    place_kernel(numbers, span, table, pieces, held)


def head_columns(kv_head, g, group):
    return slice((kv_head * group + g) * HEAD, (kv_head * group + g + 1) * HEAD)


def query_rows(q_ref, span, kv_head, group, in_order, heads):
    slots = [
        jnp.concatenate(
            [
                q_ref[slot * span : (slot + 1) * span, head_columns(kv_head, g, group)]
                for g in heads
            ],
            axis=0,
        )
        for slot in range(2)
    ]
    return jnp.where(in_order, slots[0], slots[1]), jnp.where(in_order, slots[1], slots[0])


def attend_kernel(kv_list, span, group, q_ref, table, held, sum_ref, top_ref, total_ref):
    kv_heads = (held.shape[0] - 1) // 2
    tile = TILE_SPANS * span
    tiles = held.shape[1] // tile
    middle = tiles // 2
    in_order, low_pos, high_pos = own_blocks(table)
    gap = lax.broadcasted_iota(jnp.int32, (span, tile), 1) - lax.broadcasted_iota(
        jnp.int32, (span, tile), 0
    )
    reach = low_pos // TILE_SPANS

    def masked(raw, key_tile, limit):
        keep = gap <= limit * span - key_tile * tile
        return jnp.where(keep[None], raw.reshape(-1, span, tile), -jnp.inf).reshape(raw.shape)

    def scores(query, keys):
        return lax.dot_general(
            query, keys, (((1,), (1,)), ((), ())), preferred_element_type=jnp.float32
        )

    def weighted(expo, rows_v):
        return jnp.dot(expo.astype(jnp.bfloat16), rows_v, preferred_element_type=jnp.float32)

    def top(items):
        return jnp.max(functools.reduce(jnp.maximum, items), axis=-1, keepdims=True)

    def expo_of(s, m):
        return jnp.exp2((s - m) * SCALE)

    def keys_at(kv_head, first, last):
        return held[kv_head, first * tile : last * tile, :]

    def values_at(kv_head, first, last):
        rows = slice(first * tile, last * tile)
        return jnp.concatenate([held[kv_heads + kv_head, rows, :], held[2 * kv_heads, rows, :]], 1)

    extras = []
    for j in range(1, middle):
        is_low = reach >= j
        extras.append(
            (j, is_low, jnp.where(is_low, j, tiles - j), jnp.where(is_low, low_pos, high_pos))
        )

    def score_all(kv_head, heads):
        low_q, high_q = query_rows(q_ref, span, kv_head, group, in_order, heads)
        full_s = scores(high_q, keys_at(kv_head, 0, middle + 1))
        high_s = [full_s[:, t * tile : (t + 1) * tile] for t in range(middle + 1)]
        high_s[middle] = masked(high_s[middle], middle, high_pos)
        low_s = masked(scores(low_q, keys_at(kv_head, 0, 1)), 0, low_pos)
        high_m = top(high_s)
        low_m = top([low_s])
        extra_s = []
        for j, is_low, key_tile, limit in extras:
            keys = jnp.where(
                is_low, keys_at(kv_head, j, j + 1), keys_at(kv_head, tiles - j, tiles - j + 1)
            )
            s = masked(scores(jnp.where(is_low, low_q, high_q), keys), key_tile, limit)
            m = top([s])
            low_m = jnp.where(is_low, jnp.maximum(low_m, m), low_m)
            high_m = jnp.where(is_low, high_m, jnp.maximum(high_m, m))
            extra_s.append(s)
        return high_s, low_s, extra_s, high_m, low_m

    def weigh(at, kv_head, heads, high_s, low_s, extra_s, high_m, low_m):
        high_o = weighted(
            jnp.concatenate([expo_of(s, high_m) for s in high_s], axis=1),
            values_at(kv_head, 0, middle + 1),
        )
        low_o = weighted(expo_of(low_s, low_m), values_at(kv_head, 0, 1))
        for (j, is_low, _, _), s in zip(extras, extra_s):
            rows_v = jnp.where(
                is_low, values_at(kv_head, j, j + 1), values_at(kv_head, tiles - j, tiles - j + 1)
            )
            o = weighted(expo_of(s, jnp.where(is_low, low_m, high_m)), rows_v)
            low_o = low_o + jnp.where(is_low, o, 0.0)
            high_o = high_o + jnp.where(is_low, 0.0, o)
        for side, (o, m) in enumerate(((low_o, low_m), (high_o, high_m))):
            out = slice(heads[0] * span, (heads[-1] + 1) * span)
            sum_ref[at, side, out] = o[:, :HEAD]
            total_ref[at, side, out] = o[:, HEAD:]
            top_ref[at, side, out] = jnp.broadcast_to(m, (o.shape[0], HEAD))

    cuts = max(1, CUTS - len(kv_list) + 1)
    many = -(-group // cuts)
    units = [
        (at, kv_head, range(first, min(group, first + many)))
        for at, kv_head in enumerate(kv_list)
        for first in range(0, group, many)
    ]
    scored = [score_all(kv_head, heads) for _, kv_head, heads in units]
    for unit, found in zip(units, scored):
        weigh(*unit, *found)


def finish_kernel(numbers, lacks, stages, span, group, kv_heads, q_ref, table, *refs):
    pieces = dict(zip(numbers, refs))
    states = refs[len(numbers) : len(numbers) + 3 * len(stages)]
    out_ref, ready, sems = refs[len(numbers) + 3 * len(stages) :]
    in_order, *positions = own_blocks(table)
    width = kv_heads * HEAD
    biases = []
    for lack in lacks:
        blocks = [block for number in lack for block in blocks_of(number, table)]
        lane_block = lax.broadcasted_iota(jnp.int32, (8, span * len(blocks)), 1) // span
        position = jnp.zeros(lane_block.shape, jnp.int32)
        for number, block in enumerate(blocks):
            position = jnp.where(lane_block == number, block, position)
        biases.append([jnp.where(position < pos, 0.0, -jnp.inf) for pos in positions])

    def rows_of(stage, column):
        parts = [pieces[number][:, column : column + HEAD] for number in lacks[stage]]
        return jnp.concatenate(parts, axis=0)

    where = [(stage, at) for stage, kv_list in enumerate(stages) for at in range(len(kv_list))]
    copies = []
    for kv_head, (stage, at) in enumerate(where):
        sum_ref, top_ref, total_ref = states[3 * stage : 3 * stage + 3]
        queries = query_rows(q_ref, span, kv_head, group, in_order, range(group))
        rows_k = rows_of(stage, kv_head * HEAD)
        rows_v = rows_of(stage, width + kv_head * HEAD)
        rows_v = jnp.concatenate([rows_v, jnp.ones(rows_v.shape, rows_v.dtype)], axis=1)
        normed = []
        for side in range(2):
            s = lax.dot_general(
                queries[side], rows_k, (((1,), (1,)), ((), ())), preferred_element_type=jnp.float32
            )
            s = (s.reshape(-1, 8, s.shape[1]) + biases[stage][side][None]).reshape(s.shape)
            m = top_ref[at, side]
            new_m = jnp.maximum(m, jnp.max(s, axis=-1, keepdims=True))
            wide = jnp.concatenate([new_m] * (s.shape[1] // HEAD), axis=1)
            e = jnp.exp2((s - wide) * SCALE).astype(jnp.bfloat16)
            fade = jnp.exp2((m - new_m) * SCALE)
            more = jnp.dot(e, rows_v, preferred_element_type=jnp.float32)
            o = sum_ref[at, side] * fade + more[:, :HEAD]
            l = total_ref[at, side] * fade + more[:, HEAD:]
            normed.append((o / l).astype(jnp.bfloat16))
        low, high = normed
        for slot, rows in enumerate(
            (jnp.where(in_order, low, high), jnp.where(in_order, high, low))
        ):
            for g in range(group):
                ready[slot * span : (slot + 1) * span, head_columns(kv_head, g, group)] = rows[
                    g * span : (g + 1) * span
                ]
        columns = pl.ds(kv_head * group * HEAD, group * HEAD)
        copy = pltpu.make_async_copy(ready.at[:, columns], out_ref.at[:, columns], sems.at[kv_head])
        copy.start()
        copies.append(copy)
    for copy in copies:
        copy.wait()


def attended(queries, keys, values, span_order):
    rows = queries.shape[0]
    span = rows // 2
    kv_heads = keys.shape[1] // HEAD
    group = queries.shape[1] // (kv_heads * HEAD)
    size = lax.axis_size("blk")
    far = size // CORES // 2
    count = rows * size
    vmem = pl.BlockSpec(memory_space=pltpu.VMEM)
    anywhere = pl.BlockSpec(memory_space=pltpu.HBM)
    params = pltpu.CompilerParams(vmem_limit_bytes=8 * 2**20 + 6 * count * 2 * kv_heads * HEAD)

    def call(kernel, out_shape, in_specs, **extra):
        return pl.pallas_call(
            kernel, out_shape=out_shape, in_specs=in_specs, compiler_params=params, **extra
        )

    width = keys.shape[1]
    lowest = jnp.array(-jnp.inf, keys.dtype)
    mine = jnp.maximum(
        lax.pad(keys, lowest, ((0, 0, 0), (0, width, 0))),
        lax.pad(values, lowest, ((0, 0, 0), (width, 0, 0))),
    )
    pieces = gather(mine)
    plan = [p[1:] for p in pieces]
    table_rows = -(-2 * len(plan) // LANES)
    table = call(
        functools.partial(setup_kernel, plan),
        jax.ShapeDtypeStruct((table_rows, LANES), jnp.int32),
        [vmem],
        out_specs=vmem,
    )(span_order.reshape(1, -1))
    q_held, loaded = call(
        load_kernel,
        (
            jax.ShapeDtypeStruct(queries.shape, queries.dtype),
            jax.ShapeDtypeStruct(table.shape, table.dtype),
        ),
        [vmem, vmem],
        out_specs=(vmem, vmem),
    )(table, queries)
    lacks = [
        [n for n, e in enumerate(plan) if e[0] == far or (e[0] == far - 1 and not e[3])],
        [n for n, e in enumerate(plan) if e[0] == far],
    ]
    stages = [list(range(kv_heads - 1)), list(range(kv_heads - 1, kv_heads))]
    held_shape = jax.ShapeDtypeStruct((2 * kv_heads + 1, count, HEAD), jnp.bfloat16)
    held = None
    states = []

    def place(numbers, held, source):
        kernel = (
            functools.partial(place_first, numbers, lacks[0], span)
            if held is None
            else functools.partial(place_more, numbers, span)
        )
        before = [] if held is None else [held]
        extra = {} if held is None else {"input_output_aliases": {1: 0}}
        return call(
            kernel, held_shape, [vmem] * (1 + len(before) + len(numbers)), out_specs=vmem, **extra
        )(source, *before, *[pieces[number][0] for number in numbers])

    def attend(stage, held):
        shape = jax.ShapeDtypeStruct((len(stages[stage]), 2, group * span, HEAD), jnp.float32)
        return call(
            functools.partial(attend_kernel, stages[stage], span, group),
            (shape, shape, shape),
            [vmem, vmem, vmem],
            out_specs=(vmem, vmem, vmem),
        )(q_held, table, held)

    placed = set(lacks[0])
    for step in range(2, far + 1):
        numbers = []
        for number, entry in enumerate(plan):
            ready = step == far or entry[0] < step - 1 or (entry[0] == step - 1 and entry[3])
            if ready and number not in placed:
                numbers.append(number)
        placed.update(numbers)
        held = place(numbers, held, loaded if step == far else table)
    states += attend(0, held)
    rest = [number for number in lacks[0] if number not in lacks[1]]
    held = place(rest, held, table)
    states += attend(1, held)
    numbers = lacks[0]
    return call(
        functools.partial(finish_kernel, numbers, lacks, stages, span, group, kv_heads),
        jax.ShapeDtypeStruct(queries.shape, jnp.bfloat16),
        [vmem] * (2 + len(numbers) + len(states)),
        out_specs=anywhere,
        scratch_shapes=[
            pltpu.VMEM(queries.shape, jnp.bfloat16),
            pltpu.SemaphoreType.DMA((kv_heads,)),
        ],
    )(q_held, table, *[pieces[number][0] for number in numbers], *states)


def solution(mesh):
    return jax.shard_map(
        attended,
        mesh=mesh,
        in_specs=(
            P(("parts", "blk"), None),
            P(("parts", "blk"), None),
            P(("parts", "blk"), None),
            P("parts"),
        ),
        out_specs=P(("parts", "blk"), None),
        check_vma=False,
    )
```

time: 28.8 us -> 28.4 us (0.986)
  Pallas kernels: 5.89 us -> 5.54 us
    pallas_call x6 -> x7, Pallas kernels: 5.71 us -> 5.36 us  [the longest x2 2.65 us: attend(): call(functools.partial(attend_kernel, stages[stage], span, group), (shape...]
  transfers between devices with their start and end apart: 15 -> 15, of which waited for: 4 -> 4; matrix products, arithmetic and copies ran while one was open for 0% -> 0% of each run, Pallas kernels for 14% -> 13%
where the time goes in v1:
time: 28.4 us; the launch traced here: 28.2 us
  starting transfers between devices  14.2 us (50%)
  waiting for transfers between devices  5.8 us (20%)
  Pallas kernels  5.54 us (20%)
  local copies, waits for them, and re-layouts  1.69 us (6%)
  other arithmetic  0.88 us (3%)
    ppermute x7, starting transfers between devices, send(): return lax.ppermute(array, 'blk', ring_pairs(size, sender, receiver, hops))  12 us
    ppermute x7, waiting for transfers between devices, send(): return lax.ppermute(array, 'blk', ring_pairs(size, sender, receiver, hops))  5.78 us
    pallas_call x2, Pallas kernels, attend(): call(functools.partial(attend_kernel, stages[stage], span, group), (shape...  2.65 us
    ppermute x8, starting transfers between devices, swap(): return lax.ppermute(array, 'blk', mate_pairs(size))  2.2 us
    pallas_call x1, Pallas kernels, attended(): call(functools.partial(finish_kernel, numbers, lacks, stages, span, group...  1.88 us
    unnamed x4, local copies, waits for them, and re-layouts  1.69 us
    max x1, other arithmetic, attended(): jnp.maximum(lax.pad(keys, lowest, ((0, 0, 0), (0, width, 0))), lax.pad(va...  0.88 us
    pallas_call x4, Pallas kernels, place(): call(kernel, held_shape, [vmem] * (1 + len(before) + len(numbers)), out_s...  0.83 us
  transfers between devices with their start and end apart: 15, of which 4 were waited for; matrix products, arithmetic and copies ran while one was open for 0% of the time, Pallas kernels for 13%

profile of v1, /device:TPU:0, one launch (start us, length us, event | category | flops | bytes accessed | tf_op | source)
XLA Modules:
  0.0 28.2 jit_solution(4161582692743825822)
XLA Ops:
  0.0 0.9 %pad_maximum_fusion.refs_0_ = bf16[64,1024]{1,0:T(8,128)(2,1)S(1)} fusion(bf16[64,512]{1,0:T(8,128)(2,1)} %param.6, bf16[64,512]{1,0:T(8,128)(2,1)} %param.5), kind=kLoop, calls=%fused_computation | loop fusion | flops 262144 | bytes 262144 | tf_op jit(solution)/shard_map/max | solution.py:361
  0.9 0.6 %collective-permute-start.4 = (bf16[64,1024]{1,0:T(8,128)(2,1)S(1)}, bf16[64,1024]{1,0:T(8,128)(2,1)S(1)}, u32[]{:S(2)}, u32[]{:S(2)}) collective-permute-start(bf16[64,1024]{1,0:T(8,128)(2,1)S(1)} %pad_maximum_fusion.refs_0_), channel_id=1, source_target_pairs={{0,1},{1,0},{2,3},{3,2},{4,5},{5,4},{6,7},{7,6},{8,9},{9,8},{10,11... | collective-permute-start | bytes 393224 | tf_op jit(solution)/shard_map/ppermute | solution.py:50
  1.4 2.7 %collective-permute-start = (bf16[64,1024]{1,0:T(8,128)(2,1)S(1)}, bf16[64,1024]{1,0:T(8,128)(2,1)S(1)}, u32[]{:S(2)}, u32[]{:S(2)}) collective-permute-start(bf16[64,1024]{1,0:T(8,128)(2,1)S(1)} %pad_maximum_fusion.refs_0_), channel_id=1, source_target_pairs={{0,5},{1,2},{2,1},{3,6},{4,9},{5,0},{6,3},{7,10},{8,13},{9,4},{10,... | collective-permute-start | bytes 393224 | tf_op jit(solution)/shard_map/ppermute | solution.py:53
  4.1 1.0 %collective-permute-start.5 = (bf16[64,1024]{1,0:T(8,128)(2,1)S(1)}, bf16[64,1024]{1,0:T(8,128)(2,1)S(1)}, u32[]{:S(2)}, u32[]{:S(2)}) collective-permute-start(bf16[64,1024]{1,0:T(8,128)(2,1)S(1)} %collective-permute-done.4.refs_1_), channel_id=1, source_target_pairs={{0,5},{1,2},{2,1},{3,6},{4,9},{5,0},{6,3},{7,10},{8,13},{9,4},{10,... | collective-permute-start | bytes 393224 | tf_op jit(solution)/shard_map/ppermute | solution.py:53
  5.1 1.7 %collective-permute-done.refs_2_ = bf16[64,1024]{1,0:T(8,128)(2,1)S(1)} collective-permute-done((bf16[64,1024]{1,0:T(8,128)(2,1)S(1)}, bf16[64,1024]{1,0:T(8,128)(2,1)S(1)}, u32[]{:S(2)}, u32[]{:S(2)}) %collective-permute-start) | collective-permute-done | bytes 131104 | tf_op jit(solution)/shard_map/ppermute | solution.py:53
  6.8 2.0 %collective-permute-start.1 = (bf16[64,1024]{1,0:T(8,128)(2,1)S(1)}, bf16[64,1024]{1,0:T(8,128)(2,1)S(1)}, u32[]{:S(2)}, u32[]{:S(2)}) collective-permute-start(bf16[64,1024]{1,0:T(8,128)(2,1)S(1)} %collective-permute-done.refs_2_), channel_id=1, source_target_pairs={{0,3},{1,4},{2,7},{3,0},{4,1},{5,8},{6,11},{7,2},{8,5},{9,12},{10,... | collective-permute-start | bytes 393224 | tf_op jit(solution)/shard_map/ppermute | solution.py:53
  8.8 1.1 %collective-permute-start.6 = (bf16[64,1024]{1,0:T(8,128)(2,1)S(1)}, bf16[64,1024]{1,0:T(8,128)(2,1)S(1)}, u32[]{:S(2)}, u32[]{:S(2)}) collective-permute-start(bf16[64,1024]{1,0:T(8,128)(2,1)S(1)} %collective-permute-done.5.refs_3_), channel_id=1, source_target_pairs={{0,3},{1,4},{2,7},{3,0},{4,1},{5,8},{6,11},{7,2},{8,5},{9,12},{10,... | collective-permute-start | bytes 393224 | tf_op jit(solution)/shard_map/ppermute | solution.py:53
  9.9 1.5 %collective-permute-done.1.refs_2_ = bf16[64,1024]{1,0:T(8,128)(2,1)S(1)} collective-permute-done((bf16[64,1024]{1,0:T(8,128)(2,1)S(1)}, bf16[64,1024]{1,0:T(8,128)(2,1)S(1)}, u32[]{:S(2)}, u32[]{:S(2)}) %collective-permute-start.1) | collective-permute-done | bytes 131104 | tf_op jit(solution)/shard_map/ppermute | solution.py:53
  11.4 2.1 %collective-permute-start.2 = (bf16[64,1024]{1,0:T(8,128)(2,1)S(1)}, bf16[64,1024]{1,0:T(8,128)(2,1)S(1)}, u32[]{:S(2)}, u32[]{:S(2)}) collective-permute-start(bf16[64,1024]{1,0:T(8,128)(2,1)S(1)} %collective-permute-done.1.refs_2_), channel_id=1, source_target_pairs={{0,5},{1,2},{2,1},{3,6},{4,9},{5,0},{6,3},{7,10},{8,13},{9,4},{10,... | collective-permute-start | bytes 393224 | tf_op jit(solution)/shard_map/ppermute | solution.py:53
  13.5 0.5 %collective-permute-start.12 = (bf16[64,1024]{1,0:T(8,128)(2,1)S(1)}, bf16[64,1024]{1,0:T(8,128)(2,1)S(1)}, u32[]{:S(2)}, u32[]{:S(2)}) collective-permute-start(bf16[64,1024]{1,0:T(8,128)(2,1)S(1)} %collective-permute-done.5.refs_3_), channel_id=1, source_target_pairs={{0,1},{1,0},{2,3},{3,2},{4,5},{5,4},{6,7},{7,6},{8,9},{9,8},{10,11... | collective-permute-start | bytes 393224 | tf_op jit(solution)/shard_map/ppermute | solution.py:50
  14.0 1.2 %collective-permute-start.7 = (bf16[64,1024]{1,0:T(8,128)(2,1)S(1)}, bf16[64,1024]{1,0:T(8,128)(2,1)S(1)}, u32[]{:S(2)}, u32[]{:S(2)}) collective-permute-start(bf16[64,1024]{1,0:T(8,128)(2,1)S(1)} %collective-permute-done.6.refs_3_), channel_id=1, source_target_pairs={{0,5},{1,2},{2,1},{3,6},{4,9},{5,0},{6,3},{7,10},{8,13},{9,4},{10,... | collective-permute-start | bytes 393224 | tf_op jit(solution)/shard_map/ppermute | solution.py:53
  15.2 1.0 %collective-permute-done.2.refs_2_ = bf16[64,1024]{1,0:T(8,128)(2,1)S(1)} collective-permute-done((bf16[64,1024]{1,0:T(8,128)(2,1)S(1)}, bf16[64,1024]{1,0:T(8,128)(2,1)S(1)}, u32[]{:S(2)}, u32[]{:S(2)}) %collective-permute-start.2) | collective-permute-done | bytes 131104 | tf_op jit(solution)/shard_map/ppermute | solution.py:53
  16.1 2.0 %collective-permute-start.9 = (bf16[64,1024]{1,0:T(8,128)(2,1)S(1)}, bf16[64,1024]{1,0:T(8,128)(2,1)S(1)}, u32[]{:S(2)}, u32[]{:S(2)}) collective-permute-start(bf16[64,1024]{1,0:T(8,128)(2,1)S(1)} %collective-permute-done.2.refs_2_), channel_id=1, source_target_pairs={{0,3},{1,4},{2,7},{3,0},{4,1},{5,8},{6,11},{7,2},{8,5},{9,12},{10,... | collective-permute-start | bytes 393224 | tf_op jit(solution)/shard_map/ppermute | solution.py:53
  18.1 0.5 %collective-permute-start.14 = (bf16[64,1024]{1,0:T(8,128)(2,1)S(1)}, bf16[64,1024]{1,0:T(8,128)(2,1)S(1)}, u32[]{:S(2)}, u32[]{:S(2)}) collective-permute-start(bf16[64,1024]{1,0:T(8,128)(2,1)S(1)} %collective-permute-done.6.refs_3_), channel_id=1, source_target_pairs={{0,1},{1,0},{2,3},{3,2},{4,5},{5,4},{6,7},{7,6},{8,9},{9,8},{10,11... | collective-permute-start | bytes 393224 | tf_op jit(solution)/shard_map/ppermute | solution.py:50
  18.7 0.4 %collective-permute-start.8 = (bf16[64,1024]{1,0:T(8,128)(2,1)S(1)}, bf16[64,1024]{1,0:T(8,128)(2,1)S(1)}, u32[]{:S(2)}, u32[]{:S(2)}) collective-permute-start(bf16[64,1024]{1,0:T(8,128)(2,1)S(1)} %collective-permute-done.7.refs_3_), channel_id=1, source_target_pairs={{0,1},{1,0},{2,3},{3,2},{4,5},{5,4},{6,7},{7,6},{8,9},{9,8},{10,11... | collective-permute-start | bytes 393224 | tf_op jit(solution)/shard_map/ppermute | solution.py:50
  19.2 1.6 %collective-permute-done.9.refs_2_ = bf16[64,1024]{1,0:T(8,128)(2,1)S(1)} collective-permute-done((bf16[64,1024]{1,0:T(8,128)(2,1)S(1)}, bf16[64,1024]{1,0:T(8,128)(2,1)S(1)}, u32[]{:S(2)}, u32[]{:S(2)}) %collective-permute-start.9) | collective-permute-done | bytes 131104 | tf_op jit(solution)/shard_map/ppermute | solution.py:53
  20.9 0.7 %copy-done.1 = s32[32]{0:T(128)S(1)} copy-done((s32[32]{0:T(128)S(1)}, s32[32]{0:T(128)}, u32[]{:S(2)}) %copy-start.1) | copy-done | bytes 152
  21.7 1.0 %copy-done = bf16[64,4096]{1,0:T(8,128)(2,1)S(1)} copy-done((bf16[64,4096]{1,0:T(8,128)(2,1)S(1)}, bf16[64,4096]{1,0:T(8,128)(2,1)}, u32[]{:S(2)}) %copy-start) | copy-done | bytes 524312
  22.8 0.3 shard_map.48.held_in
  23.1 0.2 shard_map.49.held_in
  23.3 0.2 shard_map.50.held.held_in
  23.5 1.8 %shard_map.51 = (f32[3,2,256,128]{3,2,1,0:T(8,128)S(1)}, f32[3,2,256,128]{3,2,1,0:T(8,128)S(1)}, f32[3,2,256,128]{3,2,1,0:T(8,128)S(1)}) custom-call(bf16[64,4096]{1,0:T(8,128)(2,1)S(1)} %get-tuple-element.13.q_ref, s32[1,128]{1,0:T(1,128)S(1)} %shard_map.46.table, bf16[9,1024,128]{2,1,0:T(8,128)(2,1)S(1)} %shard_map.50.held.held_in), custom_call_target="tpu_custom_call" | custom-call | tf_op jit(solution)/shard_map/pallas_call | solution.py:406
  25.5 0.9 %shard_map.53 = (f32[1,2,256,128]{3,2,1,0:T(8,128)S(1)}, f32[1,2,256,128]{3,2,1,0:T(8,128)S(1)}, f32[1,2,256,128]{3,2,1,0:T(8,128)S(1)}) custom-call(bf16[64,4096]{1,0:T(8,128)(2,1)S(1)} %get-tuple-element.13.q_ref, s32[1,128]{1,0:T(1,128)S(1)} %shard_map.46.table, bf16[9,1024,128]{2,1,0:T(8,128)(2,1)S(1)} %shard_map.52.held), custom_call_target="tpu_custom_call" | custom-call | tf_op jit(solution)/shard_map/pallas_call | solution.py:406
  26.4 1.9 %shard_map.54 = bf16[64,4096]{1,0:T(8,128)(2,1)} custom-call(bf16[64,4096]{1,0:T(8,128)(2,1)S(1)} %get-tuple-element.13.q_ref, s32[1,128]{1,0:T(1,128)S(1)} %shard_map.46.table, bf16[64,1024]{1,0:T(8,128)(2,1)S(1)} %collective-permute-done.3.refs_0_, bf16[64,1024]{1,0:T(8,128)(2,1)S(1)} %collective-permute-done.8.refs_1_, ...), custom_call_target="tpu_custom_call" | custom-call | tf_op jit(solution)/shard_map/pallas_call | solution.py:427
  (20 shorter events, 0.6 us)
Async XLA Ops:
  0.9 3.2 %collective-permute-start.4 = (bf16[64,1024]{1,0:T(8,128)(2,1)S(1)}, bf16[64,1024]{1,0:T(8,128)(2,1)S(1)}, u32[]{:S(2)}, u32[]{:S(2)}) collective-permute-start(bf16[64,1024]{1,0:T(8,128)(2,1)S(1)} %pad_maximum_fusion.refs_0_), channel_id=1, source_target_pairs={{0,1},{1,0},{2,3},{3,2},{4,5},{5,4},{6,7},{7,6},{8,9},{9,8},{10,11... | collective-permute-start | bytes 393224 | tf_op jit(solution)/shard_map/ppermute | solution.py:50
  1.4 5.3 %collective-permute-start = (bf16[64,1024]{1,0:T(8,128)(2,1)S(1)}, bf16[64,1024]{1,0:T(8,128)(2,1)S(1)}, u32[]{:S(2)}, u32[]{:S(2)}) collective-permute-start(bf16[64,1024]{1,0:T(8,128)(2,1)S(1)} %pad_maximum_fusion.refs_0_), channel_id=1, source_target_pairs={{0,5},{1,2},{2,1},{3,6},{4,9},{5,0},{6,3},{7,10},{8,13},{9,4},{10,... | collective-permute-start | bytes 393224 | tf_op jit(solution)/shard_map/ppermute | solution.py:53
  4.1 4.6 %collective-permute-start.5 = (bf16[64,1024]{1,0:T(8,128)(2,1)S(1)}, bf16[64,1024]{1,0:T(8,128)(2,1)S(1)}, u32[]{:S(2)}, u32[]{:S(2)}) collective-permute-start(bf16[64,1024]{1,0:T(8,128)(2,1)S(1)} %collective-permute-done.4.refs_1_), channel_id=1, source_target_pairs={{0,5},{1,2},{2,1},{3,6},{4,9},{5,0},{6,3},{7,10},{8,13},{9,4},{10,... | collective-permute-start | bytes 393224 | tf_op jit(solution)/shard_map/ppermute | solution.py:53
  6.8 4.6 %collective-permute-start.1 = (bf16[64,1024]{1,0:T(8,128)(2,1)S(1)}, bf16[64,1024]{1,0:T(8,128)(2,1)S(1)}, u32[]{:S(2)}, u32[]{:S(2)}) collective-permute-start(bf16[64,1024]{1,0:T(8,128)(2,1)S(1)} %collective-permute-done.refs_2_), channel_id=1, source_target_pairs={{0,3},{1,4},{2,7},{3,0},{4,1},{5,8},{6,11},{7,2},{8,5},{9,12},{10,... | collective-permute-start | bytes 393224 | tf_op jit(solution)/shard_map/ppermute | solution.py:53
  8.8 5.3 %collective-permute-start.6 = (bf16[64,1024]{1,0:T(8,128)(2,1)S(1)}, bf16[64,1024]{1,0:T(8,128)(2,1)S(1)}, u32[]{:S(2)}, u32[]{:S(2)}) collective-permute-start(bf16[64,1024]{1,0:T(8,128)(2,1)S(1)} %collective-permute-done.5.refs_3_), channel_id=1, source_target_pairs={{0,3},{1,4},{2,7},{3,0},{4,1},{5,8},{6,11},{7,2},{8,5},{9,12},{10,... | collective-permute-start | bytes 393224 | tf_op jit(solution)/shard_map/ppermute | solution.py:53
  11.4 4.7 %collective-permute-start.2 = (bf16[64,1024]{1,0:T(8,128)(2,1)S(1)}, bf16[64,1024]{1,0:T(8,128)(2,1)S(1)}, u32[]{:S(2)}, u32[]{:S(2)}) collective-permute-start(bf16[64,1024]{1,0:T(8,128)(2,1)S(1)} %collective-permute-done.1.refs_2_), channel_id=1, source_target_pairs={{0,5},{1,2},{2,1},{3,6},{4,9},{5,0},{6,3},{7,10},{8,13},{9,4},{10,... | collective-permute-start | bytes 393224 | tf_op jit(solution)/shard_map/ppermute | solution.py:53
  13.5 4.6 %collective-permute-start.11 = (bf16[64,1024]{1,0:T(8,128)(2,1)S(1)}, bf16[64,1024]{1,0:T(8,128)(2,1)S(1)}, u32[]{:S(2)}, u32[]{:S(2)}) collective-permute-start(bf16[64,1024]{1,0:T(8,128)(2,1)S(1)} %collective-permute-done.refs_2_), channel_id=1, source_target_pairs={{0,1},{1,0},{2,3},{3,2},{4,5},{5,4},{6,7},{7,6},{8,9},{9,8},{10,11... | collective-permute-start | bytes 393224 | tf_op jit(solution)/shard_map/ppermute | solution.py:50
  13.5 5.1 %collective-permute-start.12 = (bf16[64,1024]{1,0:T(8,128)(2,1)S(1)}, bf16[64,1024]{1,0:T(8,128)(2,1)S(1)}, u32[]{:S(2)}, u32[]{:S(2)}) collective-permute-start(bf16[64,1024]{1,0:T(8,128)(2,1)S(1)} %collective-permute-done.5.refs_3_), channel_id=1, source_target_pairs={{0,1},{1,0},{2,3},{3,2},{4,5},{5,4},{6,7},{7,6},{8,9},{9,8},{10,11... | collective-permute-start | bytes 393224 | tf_op jit(solution)/shard_map/ppermute | solution.py:50
  14.0 4.7 %collective-permute-start.7 = (bf16[64,1024]{1,0:T(8,128)(2,1)S(1)}, bf16[64,1024]{1,0:T(8,128)(2,1)S(1)}, u32[]{:S(2)}, u32[]{:S(2)}) collective-permute-start(bf16[64,1024]{1,0:T(8,128)(2,1)S(1)} %collective-permute-done.6.refs_3_), channel_id=1, source_target_pairs={{0,5},{1,2},{2,1},{3,6},{4,9},{5,0},{6,3},{7,10},{8,13},{9,4},{10,... | collective-permute-start | bytes 393224 | tf_op jit(solution)/shard_map/ppermute | solution.py:53
  16.1 4.6 %collective-permute-start.9 = (bf16[64,1024]{1,0:T(8,128)(2,1)S(1)}, bf16[64,1024]{1,0:T(8,128)(2,1)S(1)}, u32[]{:S(2)}, u32[]{:S(2)}) collective-permute-start(bf16[64,1024]{1,0:T(8,128)(2,1)S(1)} %collective-permute-done.2.refs_2_), channel_id=1, source_target_pairs={{0,3},{1,4},{2,7},{3,0},{4,1},{5,8},{6,11},{7,2},{8,5},{9,12},{10,... | collective-permute-start | bytes 393224 | tf_op jit(solution)/shard_map/ppermute | solution.py:53
  18.1 5.1 %collective-permute-start.13 = (bf16[64,1024]{1,0:T(8,128)(2,1)S(1)}, bf16[64,1024]{1,0:T(8,128)(2,1)S(1)}, u32[]{:S(2)}, u32[]{:S(2)}) collective-permute-start(bf16[64,1024]{1,0:T(8,128)(2,1)S(1)} %collective-permute-done.1.refs_2_), channel_id=1, source_target_pairs={{0,1},{1,0},{2,3},{3,2},{4,5},{5,4},{6,7},{7,6},{8,9},{9,8},{10,11... | collective-permute-start | bytes 393224 | tf_op jit(solution)/shard_map/ppermute | solution.py:50
  18.1 5.1 %collective-permute-start.14 = (bf16[64,1024]{1,0:T(8,128)(2,1)S(1)}, bf16[64,1024]{1,0:T(8,128)(2,1)S(1)}, u32[]{:S(2)}, u32[]{:S(2)}) collective-permute-start(bf16[64,1024]{1,0:T(8,128)(2,1)S(1)} %collective-permute-done.6.refs_3_), channel_id=1, source_target_pairs={{0,1},{1,0},{2,3},{3,2},{4,5},{5,4},{6,7},{7,6},{8,9},{9,8},{10,11... | collective-permute-start | bytes 393224 | tf_op jit(solution)/shard_map/ppermute | solution.py:50
  18.6 6.6 %collective-permute-start.3 = (bf16[64,1024]{1,0:T(8,128)(2,1)S(1)}, bf16[64,1024]{1,0:T(8,128)(2,1)S(1)}, u32[]{:S(2)}, u32[]{:S(2)}) collective-permute-start(bf16[64,1024]{1,0:T(8,128)(2,1)S(1)} %collective-permute-done.2.refs_2_), channel_id=1, source_target_pairs={{0,1},{1,0},{2,3},{3,2},{4,5},{5,4},{6,7},{7,6},{8,9},{9,8},{10,11... | collective-permute-start | bytes 393224 | tf_op jit(solution)/shard_map/ppermute | solution.py:50
  18.7 6.6 %collective-permute-start.8 = (bf16[64,1024]{1,0:T(8,128)(2,1)S(1)}, bf16[64,1024]{1,0:T(8,128)(2,1)S(1)}, u32[]{:S(2)}, u32[]{:S(2)}) collective-permute-start(bf16[64,1024]{1,0:T(8,128)(2,1)S(1)} %collective-permute-done.7.refs_3_), channel_id=1, source_target_pairs={{0,1},{1,0},{2,3},{3,2},{4,5},{5,4},{6,7},{7,6},{8,9},{9,8},{10,11... | collective-permute-start | bytes 393224 | tf_op jit(solution)/shard_map/ppermute | solution.py:50
  20.8 5.6 %collective-permute-start.10 = (bf16[64,1024]{1,0:T(8,128)(2,1)S(1)}, bf16[64,1024]{1,0:T(8,128)(2,1)S(1)}, u32[]{:S(2)}, u32[]{:S(2)}) collective-permute-start(bf16[64,1024]{1,0:T(8,128)(2,1)S(1)} %collective-permute-done.9.refs_2_), channel_id=1, source_target_pairs={{0,1},{1,0},{2,3},{3,2},{4,5},{5,4},{6,7},{7,6},{8,9},{9,8},{10,11... | collective-permute-start | bytes 393224 | tf_op jit(solution)/shard_map/ppermute | solution.py:50
  20.9 0.7 %copy-start.1 = (s32[32]{0:T(128)S(1)}, s32[32]{0:T(128)}, u32[]{:S(2)}) copy-start(s32[32]{0:T(128)} %param.7) | copy-start | bytes 388
  21.7 1.0 %copy-start = (bf16[64,4096]{1,0:T(8,128)(2,1)S(1)}, bf16[64,4096]{1,0:T(8,128)(2,1)}, u32[]{:S(2)}) copy-start(bf16[64,4096]{1,0:T(8,128)(2,1)} %q_ref.1) | copy-start | bytes 1572868

commit v2 on v1

--- a/solution.py
+++ b/solution.py
@@ -117,9 +117,30 @@
     table[...] = known
 
 
-def load_kernel(table, q_ref, q_out, table_out):
-    q_out[...] = q_ref[...]
-    table_out[...] = table[...]
+def place_last(numbers, early, span, table, held_in, *refs):
+    del held_in
+    *pieces, held, tail = refs
+    by_number = dict(zip(early, pieces))
+    place_kernel(numbers, span, table, [by_number[number] for number in numbers], held)
+    for spot, number in enumerate(early):
+        first, second = blocks_of(number, table)
+        ref = by_number[number]
+        for slot, side in enumerate((first > second, first < second)):
+            for part in range(tail.shape[0]):
+                tail[part, side.astype(jnp.int32), spot * span : (spot + 1) * span, :] = ref[
+                    slot * span : (slot + 1) * span, part * HEAD : (part + 1) * HEAD
+                ]
+
+
+def load_kernel(span, group, table, q_ref, q_out):
+    in_order, _, _ = own_blocks(table)
+    for kv_head in range(q_out.shape[0]):
+        for g in range(group):
+            columns = head_columns(kv_head, g, group)
+            slots = [q_ref[slot * span : (slot + 1) * span, columns] for slot in range(2)]
+            rows = slice(g * span, (g + 1) * span)
+            q_out[kv_head, 0, rows, :] = jnp.where(in_order, slots[0], slots[1])
+            q_out[kv_head, 1, rows, :] = jnp.where(in_order, slots[1], slots[0])
 
 
 def put_block(held, block, span, rows, present):
@@ -173,26 +194,12 @@
     return slice((kv_head * group + g) * HEAD, (kv_head * group + g + 1) * HEAD)
 
 
-def query_rows(q_ref, span, kv_head, group, in_order, heads):
-    slots = [
-        jnp.concatenate(
-            [
-                q_ref[slot * span : (slot + 1) * span, head_columns(kv_head, g, group)]
-                for g in heads
-            ],
-            axis=0,
-        )
-        for slot in range(2)
-    ]
-    return jnp.where(in_order, slots[0], slots[1]), jnp.where(in_order, slots[1], slots[0])
-
-
 def attend_kernel(kv_list, span, group, q_ref, table, held, sum_ref, top_ref, total_ref):
     kv_heads = (held.shape[0] - 1) // 2
     tile = TILE_SPANS * span
     tiles = held.shape[1] // tile
     middle = tiles // 2
-    in_order, low_pos, high_pos = own_blocks(table)
+    _, low_pos, high_pos = own_blocks(table)
     gap = lax.broadcasted_iota(jnp.int32, (span, tile), 1) - lax.broadcasted_iota(
         jnp.int32, (span, tile), 0
     )
@@ -231,7 +238,8 @@
         )
 
     def score_all(kv_head, heads):
-        low_q, high_q = query_rows(q_ref, span, kv_head, group, in_order, heads)
+        rows = slice(heads[0] * span, (heads[-1] + 1) * span)
+        low_q, high_q = q_ref[kv_head, 0, rows, :], q_ref[kv_head, 1, rows, :]
         full_s = scores(high_q, keys_at(kv_head, 0, middle + 1))
         high_s = [full_s[:, t * tile : (t + 1) * tile] for t in range(middle + 1)]
         high_s[middle] = masked(high_s[middle], middle, high_pos)
@@ -281,45 +289,81 @@
         weigh(*unit, *found)
 
 
-def finish_kernel(numbers, lacks, stages, span, group, kv_heads, q_ref, table, *refs):
-    pieces = dict(zip(numbers, refs))
-    states = refs[len(numbers) : len(numbers) + 3 * len(stages)]
-    out_ref, ready, sems = refs[len(numbers) + 3 * len(stages) :]
-    in_order, *positions = own_blocks(table)
-    width = kv_heads * HEAD
-    biases = []
+def finish_kernel(early, final, lacks, stages, span, group, kv_heads, q_ref, table, tail, *refs):
+    final_ref = refs[0]
+    states = refs[1 : 1 + 3 * len(stages)]
+    out_ref, ready, sems = refs[1 + 3 * len(stages) :]
+    in_order, low_pos, high_pos = own_blocks(table)
+    first, second = blocks_of(final, table)
+    final_in_order = first < second
+
+    def bias_of(blocks, limit):
+        lane_block = lax.broadcasted_iota(jnp.int32, (8, span * len(blocks)), 1) // span
+        position = jnp.full(lane_block.shape, -1, jnp.int32)
+        for number, block in enumerate(blocks):
+            if block is not None:
+                position = jnp.where(lane_block == number, block, position)
+        return jnp.where(position < limit, 0.0, -jnp.inf)
+
+    spots, biases = [], []
     for lack in lacks:
-        blocks = [block for number in lack for block in blocks_of(number, table)]
-        lane_block = lax.broadcasted_iota(jnp.int32, (8, span * len(blocks)), 1) // span
-        position = jnp.zeros(lane_block.shape, jnp.int32)
-        for number, block in enumerate(blocks):
-            position = jnp.where(lane_block == number, block, position)
-        biases.append([jnp.where(position < pos, 0.0, -jnp.inf) for pos in positions])
-
-    def rows_of(stage, column):
-        parts = [pieces[number][:, column : column + HEAD] for number in lacks[stage]]
-        return jnp.concatenate(parts, axis=0)
+        held_first = min(early.index(number) for number in lack if number != final)
+        ordered = early[held_first:] + [final]
+        pairs = [blocks_of(number, table) for number in ordered]
+        lower = [jnp.minimum(*pair) for pair in pairs]
+        higher = [jnp.maximum(*pair) for pair in pairs]
+        spots.append(held_first * span)
+        biases.append((bias_of(lower, low_pos), bias_of([None] * len(lower) + higher, high_pos)))
+
+    def rows_of(stage, part):
+        columns = slice(part * HEAD, (part + 1) * HEAD)
+        slots = [final_ref[slot * span : (slot + 1) * span, columns] for slot in range(2)]
+        low = jnp.where(final_in_order, slots[0], slots[1])
+        high = jnp.where(final_in_order, slots[1], slots[0])
+        start = spots[stage]
+        return (
+            jnp.concatenate([tail[part, 0, start:, :], low], axis=0),
+            jnp.concatenate([tail[part, 1, start:, :], high], axis=0),
+        )
 
     where = [(stage, at) for stage, kv_list in enumerate(stages) for at in range(len(kv_list))]
-    copies = []
-    for kv_head, (stage, at) in enumerate(where):
-        sum_ref, top_ref, total_ref = states[3 * stage : 3 * stage + 3]
-        queries = query_rows(q_ref, span, kv_head, group, in_order, range(group))
-        rows_k = rows_of(stage, kv_head * HEAD)
-        rows_v = rows_of(stage, width + kv_head * HEAD)
-        rows_v = jnp.concatenate([rows_v, jnp.ones(rows_v.shape, rows_v.dtype)], axis=1)
-        normed = []
+
+    def score(kv_head):
+        stage, at = where[kv_head]
+        low_k, high_k = rows_of(stage, kv_head)
+        keys = (low_k, jnp.concatenate([low_k, high_k], axis=0))
+        found = []
         for side in range(2):
             s = lax.dot_general(
-                queries[side], rows_k, (((1,), (1,)), ((), ())), preferred_element_type=jnp.float32
+                q_ref[kv_head, side],
+                keys[side],
+                (((1,), (1,)), ((), ())),
+                preferred_element_type=jnp.float32,
             )
-            s = (s.reshape(-1, 8, s.shape[1]) + biases[stage][side][None]).reshape(s.shape)
-            m = top_ref[at, side]
-            new_m = jnp.maximum(m, jnp.max(s, axis=-1, keepdims=True))
-            wide = jnp.concatenate([new_m] * (s.shape[1] // HEAD), axis=1)
+            bias = biases[stage][side]
+            clear = low_k.shape[0] if side and low_k.shape[0] % HEAD == 0 else 0
+            part = s[:, clear:]
+            part = (part.reshape(-1, 8, part.shape[1]) + bias[None, :, clear:]).reshape(part.shape)
+            s = jnp.concatenate([s[:, :clear], part], axis=1) if clear else part
+            new_m = jnp.maximum(
+                states[3 * stage + 1][at, side], jnp.max(s, axis=-1, keepdims=True)
+            )
+            wide = jnp.concatenate([new_m] * -(-s.shape[1] // HEAD), axis=1)[:, : s.shape[1]]
             e = jnp.exp2((s - wide) * SCALE).astype(jnp.bfloat16)
-            fade = jnp.exp2((m - new_m) * SCALE)
-            more = jnp.dot(e, rows_v, preferred_element_type=jnp.float32)
+            found.append((e, new_m))
+        return found
+
+    def merge(kv_head, found):
+        stage, at = where[kv_head]
+        sum_ref, top_ref, total_ref = states[3 * stage : 3 * stage + 3]
+        low_v, high_v = rows_of(stage, kv_heads + kv_head)
+        low_v = jnp.concatenate([low_v, jnp.ones(low_v.shape, low_v.dtype)], axis=1)
+        high_v = jnp.concatenate([high_v, jnp.ones(high_v.shape, high_v.dtype)], axis=1)
+        rows_v = (low_v, jnp.concatenate([low_v, high_v], axis=0))
+        normed = []
+        for side, (e, new_m) in enumerate(found):
+            fade = jnp.exp2((top_ref[at, side] - new_m) * SCALE)
+            more = jnp.dot(e, rows_v[side], preferred_element_type=jnp.float32)
             o = sum_ref[at, side] * fade + more[:, :HEAD]
             l = total_ref[at, side] * fade + more[:, HEAD:]
             normed.append((o / l).astype(jnp.bfloat16))
@@ -334,7 +378,10 @@
         columns = pl.ds(kv_head * group * HEAD, group * HEAD)
         copy = pltpu.make_async_copy(ready.at[:, columns], out_ref.at[:, columns], sems.at[kv_head])
         copy.start()
-        copies.append(copy)
+        return copy
+
+    scored = [score(kv_head) for kv_head in range(kv_heads)]
+    copies = [merge(kv_head, scored[kv_head]) for kv_head in range(kv_heads)]
     for copy in copies:
         copy.wait()
 
@@ -371,14 +418,11 @@
         [vmem],
         out_specs=vmem,
     )(span_order.reshape(1, -1))
-    q_held, loaded = call(
-        load_kernel,
-        (
-            jax.ShapeDtypeStruct(queries.shape, queries.dtype),
-            jax.ShapeDtypeStruct(table.shape, table.dtype),
-        ),
+    q_held = call(
+        functools.partial(load_kernel, span, group),
+        jax.ShapeDtypeStruct((kv_heads, 2, group * span, HEAD), queries.dtype),
         [vmem, vmem],
-        out_specs=(vmem, vmem),
+        out_specs=vmem,
     )(table, queries)
     lacks = [
         [n for n, e in enumerate(plan) if e[0] == far or (e[0] == far - 1 and not e[3])],
@@ -389,7 +433,7 @@
     held = None
     states = []
 
-    def place(numbers, held, source):
+    def place(numbers, held):
         kernel = (
             functools.partial(place_first, numbers, lacks[0], span)
             if held is None
@@ -399,7 +443,7 @@
         extra = {} if held is None else {"input_output_aliases": {1: 0}}
         return call(
             kernel, held_shape, [vmem] * (1 + len(before) + len(numbers)), out_specs=vmem, **extra
-        )(source, *before, *[pieces[number][0] for number in numbers])
+        )(table, *before, *[pieces[number][0] for number in numbers])
 
     def attend(stage, held):
         shape = jax.ShapeDtypeStruct((len(stages[stage]), 2, group * span, HEAD), jnp.float32)
@@ -418,22 +462,32 @@
             if ready and number not in placed:
                 numbers.append(number)
         placed.update(numbers)
-        held = place(numbers, held, loaded if step == far else table)
+        held = place(numbers, held)
     states += attend(0, held)
     rest = [number for number in lacks[0] if number not in lacks[1]]
-    held = place(rest, held, table)
+    final = next(number for number in lacks[1] if not plan[number][3])
+    early = rest + [number for number in lacks[1] if number != final]
+    held, tail = call(
+        functools.partial(place_last, rest, early, span),
+        (
+            held_shape,
+            jax.ShapeDtypeStruct((2 * kv_heads, 2, len(early) * span, HEAD), jnp.bfloat16),
+        ),
+        [vmem] * (2 + len(early)),
+        out_specs=(vmem, vmem),
+        input_output_aliases={1: 0},
+    )(table, held, *[pieces[number][0] for number in early])
     states += attend(1, held)
-    numbers = lacks[0]
     return call(
-        functools.partial(finish_kernel, numbers, lacks, stages, span, group, kv_heads),
+        functools.partial(finish_kernel, early, final, lacks, stages, span, group, kv_heads),
         jax.ShapeDtypeStruct(queries.shape, jnp.bfloat16),
-        [vmem] * (2 + len(numbers) + len(states)),
+        [vmem] * (4 + len(states)),
         out_specs=anywhere,
         scratch_shapes=[
             pltpu.VMEM(queries.shape, jnp.bfloat16),
             pltpu.SemaphoreType.DMA((kv_heads,)),
         ],
-    )(q_held, table, *[pieces[number][0] for number in numbers], *states)
+    )(q_held, table, tail, pieces[final][0], *states)
 
 
 def solution(mesh):

time: 28.4 us -> 28.4 us (level)
    pallas_call x2 -> x3, Pallas kernels: 1.92 us -> 2.16 us  [the longest x1 1.76 us: attended(): call(functools.partial(finish_kernel, early, final, lacks, stages, span,...]
    pallas_call x4 -> x3, Pallas kernels: 0.83 us -> 0.68 us  [place(): call(kernel, held_shape, [vmem] * (1 + len(before) + len(numbers)), out_s...]
where the time goes in v2:
time: 28.4 us; the launch traced here: 28.2 us
  starting transfers between devices  14.2 us (50%)
  waiting for transfers between devices  5.8 us (20%)
  Pallas kernels  5.53 us (19%)
  local copies, waits for them, and re-layouts  1.69 us (6%)
  other arithmetic  0.88 us (3%)
    ppermute x7, starting transfers between devices, send(): return lax.ppermute(array, 'blk', ring_pairs(size, sender, receiver, hops))  12 us
    ppermute x7, waiting for transfers between devices, send(): return lax.ppermute(array, 'blk', ring_pairs(size, sender, receiver, hops))  5.78 us
    pallas_call x2, Pallas kernels, attend(): call(functools.partial(attend_kernel, stages[stage], span, group), (shape...  2.55 us
    ppermute x8, starting transfers between devices, swap(): return lax.ppermute(array, 'blk', mate_pairs(size))  2.2 us
    pallas_call x1, Pallas kernels, attended(): call(functools.partial(finish_kernel, early, final, lacks, stages, span,...  1.76 us
    unnamed x4, local copies, waits for them, and re-layouts  1.69 us
    max x1, other arithmetic, attended(): jnp.maximum(lax.pad(keys, lowest, ((0, 0, 0), (0, width, 0))), lax.pad(va...  0.88 us
    pallas_call x3, Pallas kernels, place(): call(kernel, held_shape, [vmem] * (1 + len(before) + len(numbers)), out_s...  0.68 us
  transfers between devices with their start and end apart: 15, of which 4 were waited for; matrix products, arithmetic and copies ran while one was open for 0% of the time, Pallas kernels for 13%

profile of v2, /device:TPU:0, one launch (start us, length us, event | category | flops | bytes accessed | tf_op | source)
XLA Modules:
  0.0 28.2 jit_solution(1339026204493850431)
XLA Ops:
  0.0 0.9 %pad_maximum_fusion.refs_0_ = bf16[64,1024]{1,0:T(8,128)(2,1)S(1)} fusion(bf16[64,512]{1,0:T(8,128)(2,1)} %param.6, bf16[64,512]{1,0:T(8,128)(2,1)} %param.5), kind=kLoop, calls=%fused_computation | loop fusion | flops 262144 | bytes 262144 | tf_op jit(solution)/shard_map/max | solution.py:408
  0.9 0.6 %collective-permute-start = (bf16[64,1024]{1,0:T(8,128)(2,1)S(1)}, bf16[64,1024]{1,0:T(8,128)(2,1)S(1)}, u32[]{:S(2)}, u32[]{:S(2)}) collective-permute-start(bf16[64,1024]{1,0:T(8,128)(2,1)S(1)} %pad_maximum_fusion.refs_0_), channel_id=1, source_target_pairs={{0,1},{1,0},{2,3},{3,2},{4,5},{5,4},{6,7},{7,6},{8,9},{9,8},{10,11... | collective-permute-start | bytes 393224 | tf_op jit(solution)/shard_map/ppermute | solution.py:50
  1.4 2.7 %collective-permute-start.1 = (bf16[64,1024]{1,0:T(8,128)(2,1)S(1)}, bf16[64,1024]{1,0:T(8,128)(2,1)S(1)}, u32[]{:S(2)}, u32[]{:S(2)}) collective-permute-start(bf16[64,1024]{1,0:T(8,128)(2,1)S(1)} %pad_maximum_fusion.refs_0_), channel_id=1, source_target_pairs={{0,5},{1,2},{2,1},{3,6},{4,9},{5,0},{6,3},{7,10},{8,13},{9,4},{10,... | collective-permute-start | bytes 393224 | tf_op jit(solution)/shard_map/ppermute | solution.py:53
  4.1 1.0 %collective-permute-start.2 = (bf16[64,1024]{1,0:T(8,128)(2,1)S(1)}, bf16[64,1024]{1,0:T(8,128)(2,1)S(1)}, u32[]{:S(2)}, u32[]{:S(2)}) collective-permute-start(bf16[64,1024]{1,0:T(8,128)(2,1)S(1)} %collective-permute-done.refs_1_), channel_id=1, source_target_pairs={{0,5},{1,2},{2,1},{3,6},{4,9},{5,0},{6,3},{7,10},{8,13},{9,4},{10,... | collective-permute-start | bytes 393224 | tf_op jit(solution)/shard_map/ppermute | solution.py:53
  5.1 1.7 %collective-permute-done.1.refs_2_ = bf16[64,1024]{1,0:T(8,128)(2,1)S(1)} collective-permute-done((bf16[64,1024]{1,0:T(8,128)(2,1)S(1)}, bf16[64,1024]{1,0:T(8,128)(2,1)S(1)}, u32[]{:S(2)}, u32[]{:S(2)}) %collective-permute-start.1) | collective-permute-done | bytes 131104 | tf_op jit(solution)/shard_map/ppermute | solution.py:53
  6.8 2.0 %collective-permute-start.5 = (bf16[64,1024]{1,0:T(8,128)(2,1)S(1)}, bf16[64,1024]{1,0:T(8,128)(2,1)S(1)}, u32[]{:S(2)}, u32[]{:S(2)}) collective-permute-start(bf16[64,1024]{1,0:T(8,128)(2,1)S(1)} %collective-permute-done.1.refs_2_), channel_id=1, source_target_pairs={{0,3},{1,4},{2,7},{3,0},{4,1},{5,8},{6,11},{7,2},{8,5},{9,12},{10,... | collective-permute-start | bytes 393224 | tf_op jit(solution)/shard_map/ppermute | solution.py:53
  8.8 1.1 %collective-permute-start.6 = (bf16[64,1024]{1,0:T(8,128)(2,1)S(1)}, bf16[64,1024]{1,0:T(8,128)(2,1)S(1)}, u32[]{:S(2)}, u32[]{:S(2)}) collective-permute-start(bf16[64,1024]{1,0:T(8,128)(2,1)S(1)} %collective-permute-done.2.refs_3_), channel_id=1, source_target_pairs={{0,3},{1,4},{2,7},{3,0},{4,1},{5,8},{6,11},{7,2},{8,5},{9,12},{10,... | collective-permute-start | bytes 393224 | tf_op jit(solution)/shard_map/ppermute | solution.py:53
  9.9 1.5 %collective-permute-done.5.refs_2_ = bf16[64,1024]{1,0:T(8,128)(2,1)S(1)} collective-permute-done((bf16[64,1024]{1,0:T(8,128)(2,1)S(1)}, bf16[64,1024]{1,0:T(8,128)(2,1)S(1)}, u32[]{:S(2)}, u32[]{:S(2)}) %collective-permute-start.5) | collective-permute-done | bytes 131104 | tf_op jit(solution)/shard_map/ppermute | solution.py:53
  11.4 2.1 %collective-permute-start.9 = (bf16[64,1024]{1,0:T(8,128)(2,1)S(1)}, bf16[64,1024]{1,0:T(8,128)(2,1)S(1)}, u32[]{:S(2)}, u32[]{:S(2)}) collective-permute-start(bf16[64,1024]{1,0:T(8,128)(2,1)S(1)} %collective-permute-done.5.refs_2_), channel_id=1, source_target_pairs={{0,5},{1,2},{2,1},{3,6},{4,9},{5,0},{6,3},{7,10},{8,13},{9,4},{10,... | collective-permute-start | bytes 393224 | tf_op jit(solution)/shard_map/ppermute | solution.py:53
  13.5 0.5 %collective-permute-start.4 = (bf16[64,1024]{1,0:T(8,128)(2,1)S(1)}, bf16[64,1024]{1,0:T(8,128)(2,1)S(1)}, u32[]{:S(2)}, u32[]{:S(2)}) collective-permute-start(bf16[64,1024]{1,0:T(8,128)(2,1)S(1)} %collective-permute-done.2.refs_3_), channel_id=1, source_target_pairs={{0,1},{1,0},{2,3},{3,2},{4,5},{5,4},{6,7},{7,6},{8,9},{9,8},{10,11... | collective-permute-start | bytes 393224 | tf_op jit(solution)/shard_map/ppermute | solution.py:50
  14.0 1.2 %collective-permute-start.10 = (bf16[64,1024]{1,0:T(8,128)(2,1)S(1)}, bf16[64,1024]{1,0:T(8,128)(2,1)S(1)}, u32[]{:S(2)}, u32[]{:S(2)}) collective-permute-start(bf16[64,1024]{1,0:T(8,128)(2,1)S(1)} %collective-permute-done.6.refs_3_), channel_id=1, source_target_pairs={{0,5},{1,2},{2,1},{3,6},{4,9},{5,0},{6,3},{7,10},{8,13},{9,4},{10,... | collective-permute-start | bytes 393224 | tf_op jit(solution)/shard_map/ppermute | solution.py:53
  15.2 1.0 %collective-permute-done.9.refs_2_ = bf16[64,1024]{1,0:T(8,128)(2,1)S(1)} collective-permute-done((bf16[64,1024]{1,0:T(8,128)(2,1)S(1)}, bf16[64,1024]{1,0:T(8,128)(2,1)S(1)}, u32[]{:S(2)}, u32[]{:S(2)}) %collective-permute-start.9) | collective-permute-done | bytes 131104 | tf_op jit(solution)/shard_map/ppermute | solution.py:53
  16.1 2.0 %collective-permute-start.13 = (bf16[64,1024]{1,0:T(8,128)(2,1)S(1)}, bf16[64,1024]{1,0:T(8,128)(2,1)S(1)}, u32[]{:S(2)}, u32[]{:S(2)}) collective-permute-start(bf16[64,1024]{1,0:T(8,128)(2,1)S(1)} %collective-permute-done.9.refs_2_), channel_id=1, source_target_pairs={{0,3},{1,4},{2,7},{3,0},{4,1},{5,8},{6,11},{7,2},{8,5},{9,12},{10,... | collective-permute-start | bytes 393224 | tf_op jit(solution)/shard_map/ppermute | solution.py:53
  18.1 0.5 %collective-permute-start.8 = (bf16[64,1024]{1,0:T(8,128)(2,1)S(1)}, bf16[64,1024]{1,0:T(8,128)(2,1)S(1)}, u32[]{:S(2)}, u32[]{:S(2)}) collective-permute-start(bf16[64,1024]{1,0:T(8,128)(2,1)S(1)} %collective-permute-done.6.refs_3_), channel_id=1, source_target_pairs={{0,1},{1,0},{2,3},{3,2},{4,5},{5,4},{6,7},{7,6},{8,9},{9,8},{10,11... | collective-permute-start | bytes 393224 | tf_op jit(solution)/shard_map/ppermute | solution.py:50
  18.7 0.4 %collective-permute-start.12 = (bf16[64,1024]{1,0:T(8,128)(2,1)S(1)}, bf16[64,1024]{1,0:T(8,128)(2,1)S(1)}, u32[]{:S(2)}, u32[]{:S(2)}) collective-permute-start(bf16[64,1024]{1,0:T(8,128)(2,1)S(1)} %collective-permute-done.10.refs_3_), channel_id=1, source_target_pairs={{0,1},{1,0},{2,3},{3,2},{4,5},{5,4},{6,7},{7,6},{8,9},{9,8},{10,11... | collective-permute-start | bytes 393224 | tf_op jit(solution)/shard_map/ppermute | solution.py:50
  19.2 1.6 %collective-permute-done.13.refs_2_ = bf16[64,1024]{1,0:T(8,128)(2,1)S(1)} collective-permute-done((bf16[64,1024]{1,0:T(8,128)(2,1)S(1)}, bf16[64,1024]{1,0:T(8,128)(2,1)S(1)}, u32[]{:S(2)}, u32[]{:S(2)}) %collective-permute-start.13) | collective-permute-done | bytes 131104 | tf_op jit(solution)/shard_map/ppermute | solution.py:53
  20.9 0.7 %copy-done.1 = s32[32]{0:T(128)S(1)} copy-done((s32[32]{0:T(128)S(1)}, s32[32]{0:T(128)}, u32[]{:S(2)}) %copy-start.1) | copy-done | bytes 152
  21.7 1.0 %copy-done = bf16[64,4096]{1,0:T(8,128)(2,1)S(1)} copy-done((bf16[64,4096]{1,0:T(8,128)(2,1)S(1)}, bf16[64,4096]{1,0:T(8,128)(2,1)}, u32[]{:S(2)}) %copy-start) | copy-done | bytes 524312
  22.9 0.3 shard_map.48.held_in
  23.2 0.2 shard_map.49.held_in
  23.7 1.7 %shard_map.52 = (f32[3,2,256,128]{3,2,1,0:T(8,128)S(1)}, f32[3,2,256,128]{3,2,1,0:T(8,128)S(1)}, f32[3,2,256,128]{3,2,1,0:T(8,128)S(1)}) custom-call(bf16[4,2,256,128]{3,2,1,0:T(8,128)(2,1)S(1)} %shard_map.47.q_ref, s32[1,128]{1,0:T(1,128)S(1)} %shard_map.46.table, bf16[9,1024,128]{2,1,0:T(8,128)(2,1)S(1)} %shard_map.50.held_in.held), custom_call_target="tpu_custom_call" | custom-call | tf_op jit(solution)/shard_map/pallas_call | solution.py:450
  25.4 0.2 shard_map.51
  25.6 0.8 %shard_map.53 = (f32[1,2,256,128]{3,2,1,0:T(8,128)S(1)}, f32[1,2,256,128]{3,2,1,0:T(8,128)S(1)}, f32[1,2,256,128]{3,2,1,0:T(8,128)S(1)}) custom-call(bf16[4,2,256,128]{3,2,1,0:T(8,128)(2,1)S(1)} %shard_map.47.q_ref, s32[1,128]{1,0:T(1,128)S(1)} %shard_map.46.table, bf16[9,1024,128]{2,1,0:T(8,128)(2,1)S(1)} %get-tuple-element.17.held), custom_call_target="tpu_custom_call" | custom-call | tf_op jit(solution)/shard_map/pallas_call | solution.py:450
  26.5 1.8 %shard_map.54 = bf16[64,4096]{1,0:T(8,128)(2,1)} custom-call(bf16[4,2,256,128]{3,2,1,0:T(8,128)(2,1)S(1)} %shard_map.47.q_ref, s32[1,128]{1,0:T(1,128)S(1)} %shard_map.46.table, bf16[8,2,96,128]{3,2,1,0:T(8,128)(2,1)S(1)} %get-tuple-element.13.tail, bf16[64,1024]{1,0:T(8,128)(2,1)S(1)} %collective-permute-done.14.refs_0_, ...), custom_call_target="tpu_custom_call" | custom-call | tf_op jit(solution)/shard_map/pallas_call | solution.py:481
  (20 shorter events, 0.8 us)
Async XLA Ops:
  0.9 3.2 %collective-permute-start = (bf16[64,1024]{1,0:T(8,128)(2,1)S(1)}, bf16[64,1024]{1,0:T(8,128)(2,1)S(1)}, u32[]{:S(2)}, u32[]{:S(2)}) collective-permute-start(bf16[64,1024]{1,0:T(8,128)(2,1)S(1)} %pad_maximum_fusion.refs_0_), channel_id=1, source_target_pairs={{0,1},{1,0},{2,3},{3,2},{4,5},{5,4},{6,7},{7,6},{8,9},{9,8},{10,11... | collective-permute-start | bytes 393224 | tf_op jit(solution)/shard_map/ppermute | solution.py:50
  1.4 5.3 %collective-permute-start.1 = (bf16[64,1024]{1,0:T(8,128)(2,1)S(1)}, bf16[64,1024]{1,0:T(8,128)(2,1)S(1)}, u32[]{:S(2)}, u32[]{:S(2)}) collective-permute-start(bf16[64,1024]{1,0:T(8,128)(2,1)S(1)} %pad_maximum_fusion.refs_0_), channel_id=1, source_target_pairs={{0,5},{1,2},{2,1},{3,6},{4,9},{5,0},{6,3},{7,10},{8,13},{9,4},{10,... | collective-permute-start | bytes 393224 | tf_op jit(solution)/shard_map/ppermute | solution.py:53
  4.1 4.6 %collective-permute-start.2 = (bf16[64,1024]{1,0:T(8,128)(2,1)S(1)}, bf16[64,1024]{1,0:T(8,128)(2,1)S(1)}, u32[]{:S(2)}, u32[]{:S(2)}) collective-permute-start(bf16[64,1024]{1,0:T(8,128)(2,1)S(1)} %collective-permute-done.refs_1_), channel_id=1, source_target_pairs={{0,5},{1,2},{2,1},{3,6},{4,9},{5,0},{6,3},{7,10},{8,13},{9,4},{10,... | collective-permute-start | bytes 393224 | tf_op jit(solution)/shard_map/ppermute | solution.py:53
  6.8 4.6 %collective-permute-start.5 = (bf16[64,1024]{1,0:T(8,128)(2,1)S(1)}, bf16[64,1024]{1,0:T(8,128)(2,1)S(1)}, u32[]{:S(2)}, u32[]{:S(2)}) collective-permute-start(bf16[64,1024]{1,0:T(8,128)(2,1)S(1)} %collective-permute-done.1.refs_2_), channel_id=1, source_target_pairs={{0,3},{1,4},{2,7},{3,0},{4,1},{5,8},{6,11},{7,2},{8,5},{9,12},{10,... | collective-permute-start | bytes 393224 | tf_op jit(solution)/shard_map/ppermute | solution.py:53
  8.8 5.3 %collective-permute-start.6 = (bf16[64,1024]{1,0:T(8,128)(2,1)S(1)}, bf16[64,1024]{1,0:T(8,128)(2,1)S(1)}, u32[]{:S(2)}, u32[]{:S(2)}) collective-permute-start(bf16[64,1024]{1,0:T(8,128)(2,1)S(1)} %collective-permute-done.2.refs_3_), channel_id=1, source_target_pairs={{0,3},{1,4},{2,7},{3,0},{4,1},{5,8},{6,11},{7,2},{8,5},{9,12},{10,... | collective-permute-start | bytes 393224 | tf_op jit(solution)/shard_map/ppermute | solution.py:53
  11.4 4.7 %collective-permute-start.9 = (bf16[64,1024]{1,0:T(8,128)(2,1)S(1)}, bf16[64,1024]{1,0:T(8,128)(2,1)S(1)}, u32[]{:S(2)}, u32[]{:S(2)}) collective-permute-start(bf16[64,1024]{1,0:T(8,128)(2,1)S(1)} %collective-permute-done.5.refs_2_), channel_id=1, source_target_pairs={{0,5},{1,2},{2,1},{3,6},{4,9},{5,0},{6,3},{7,10},{8,13},{9,4},{10,... | collective-permute-start | bytes 393224 | tf_op jit(solution)/shard_map/ppermute | solution.py:53
  13.5 4.6 %collective-permute-start.3 = (bf16[64,1024]{1,0:T(8,128)(2,1)S(1)}, bf16[64,1024]{1,0:T(8,128)(2,1)S(1)}, u32[]{:S(2)}, u32[]{:S(2)}) collective-permute-start(bf16[64,1024]{1,0:T(8,128)(2,1)S(1)} %collective-permute-done.1.refs_2_), channel_id=1, source_target_pairs={{0,1},{1,0},{2,3},{3,2},{4,5},{5,4},{6,7},{7,6},{8,9},{9,8},{10,11... | collective-permute-start | bytes 393224 | tf_op jit(solution)/shard_map/ppermute | solution.py:50
  13.5 5.1 %collective-permute-start.4 = (bf16[64,1024]{1,0:T(8,128)(2,1)S(1)}, bf16[64,1024]{1,0:T(8,128)(2,1)S(1)}, u32[]{:S(2)}, u32[]{:S(2)}) collective-permute-start(bf16[64,1024]{1,0:T(8,128)(2,1)S(1)} %collective-permute-done.2.refs_3_), channel_id=1, source_target_pairs={{0,1},{1,0},{2,3},{3,2},{4,5},{5,4},{6,7},{7,6},{8,9},{9,8},{10,11... | collective-permute-start | bytes 393224 | tf_op jit(solution)/shard_map/ppermute | solution.py:50
  14.0 4.7 %collective-permute-start.10 = (bf16[64,1024]{1,0:T(8,128)(2,1)S(1)}, bf16[64,1024]{1,0:T(8,128)(2,1)S(1)}, u32[]{:S(2)}, u32[]{:S(2)}) collective-permute-start(bf16[64,1024]{1,0:T(8,128)(2,1)S(1)} %collective-permute-done.6.refs_3_), channel_id=1, source_target_pairs={{0,5},{1,2},{2,1},{3,6},{4,9},{5,0},{6,3},{7,10},{8,13},{9,4},{10,... | collective-permute-start | bytes 393224 | tf_op jit(solution)/shard_map/ppermute | solution.py:53
  16.1 4.6 %collective-permute-start.13 = (bf16[64,1024]{1,0:T(8,128)(2,1)S(1)}, bf16[64,1024]{1,0:T(8,128)(2,1)S(1)}, u32[]{:S(2)}, u32[]{:S(2)}) collective-permute-start(bf16[64,1024]{1,0:T(8,128)(2,1)S(1)} %collective-permute-done.9.refs_2_), channel_id=1, source_target_pairs={{0,3},{1,4},{2,7},{3,0},{4,1},{5,8},{6,11},{7,2},{8,5},{9,12},{10,... | collective-permute-start | bytes 393224 | tf_op jit(solution)/shard_map/ppermute | solution.py:53
  18.1 5.3 %collective-permute-start.7 = (bf16[64,1024]{1,0:T(8,128)(2,1)S(1)}, bf16[64,1024]{1,0:T(8,128)(2,1)S(1)}, u32[]{:S(2)}, u32[]{:S(2)}) collective-permute-start(bf16[64,1024]{1,0:T(8,128)(2,1)S(1)} %collective-permute-done.5.refs_2_), channel_id=1, source_target_pairs={{0,1},{1,0},{2,3},{3,2},{4,5},{5,4},{6,7},{7,6},{8,9},{9,8},{10,11... | collective-permute-start | bytes 393224 | tf_op jit(solution)/shard_map/ppermute | solution.py:50
  18.1 5.3 %collective-permute-start.8 = (bf16[64,1024]{1,0:T(8,128)(2,1)S(1)}, bf16[64,1024]{1,0:T(8,128)(2,1)S(1)}, u32[]{:S(2)}, u32[]{:S(2)}) collective-permute-start(bf16[64,1024]{1,0:T(8,128)(2,1)S(1)} %collective-permute-done.6.refs_3_), channel_id=1, source_target_pairs={{0,1},{1,0},{2,3},{3,2},{4,5},{5,4},{6,7},{7,6},{8,9},{9,8},{10,11... | collective-permute-start | bytes 393224 | tf_op jit(solution)/shard_map/ppermute | solution.py:50
  18.6 6.7 %collective-permute-start.11 = (bf16[64,1024]{1,0:T(8,128)(2,1)S(1)}, bf16[64,1024]{1,0:T(8,128)(2,1)S(1)}, u32[]{:S(2)}, u32[]{:S(2)}) collective-permute-start(bf16[64,1024]{1,0:T(8,128)(2,1)S(1)} %collective-permute-done.9.refs_2_), channel_id=1, source_target_pairs={{0,1},{1,0},{2,3},{3,2},{4,5},{5,4},{6,7},{7,6},{8,9},{9,8},{10,11... | collective-permute-start | bytes 393224 | tf_op jit(solution)/shard_map/ppermute | solution.py:50
  18.7 6.7 %collective-permute-start.12 = (bf16[64,1024]{1,0:T(8,128)(2,1)S(1)}, bf16[64,1024]{1,0:T(8,128)(2,1)S(1)}, u32[]{:S(2)}, u32[]{:S(2)}) collective-permute-start(bf16[64,1024]{1,0:T(8,128)(2,1)S(1)} %collective-permute-done.10.refs_3_), channel_id=1, source_target_pairs={{0,1},{1,0},{2,3},{3,2},{4,5},{5,4},{6,7},{7,6},{8,9},{9,8},{10,11... | collective-permute-start | bytes 393224 | tf_op jit(solution)/shard_map/ppermute | solution.py:50
  20.8 5.7 %collective-permute-start.14 = (bf16[64,1024]{1,0:T(8,128)(2,1)S(1)}, bf16[64,1024]{1,0:T(8,128)(2,1)S(1)}, u32[]{:S(2)}, u32[]{:S(2)}) collective-permute-start(bf16[64,1024]{1,0:T(8,128)(2,1)S(1)} %collective-permute-done.13.refs_2_), channel_id=1, source_target_pairs={{0,1},{1,0},{2,3},{3,2},{4,5},{5,4},{6,7},{7,6},{8,9},{9,8},{10,11... | collective-permute-start | bytes 393224 | tf_op jit(solution)/shard_map/ppermute | solution.py:50
  20.9 0.7 %copy-start.1 = (s32[32]{0:T(128)S(1)}, s32[32]{0:T(128)}, u32[]{:S(2)}) copy-start(s32[32]{0:T(128)} %param.7) | copy-start | bytes 388
  21.7 1.0 %copy-start = (bf16[64,4096]{1,0:T(8,128)(2,1)S(1)}, bf16[64,4096]{1,0:T(8,128)(2,1)}, u32[]{:S(2)}) copy-start(bf16[64,4096]{1,0:T(8,128)(2,1)} %q_ref.1) | copy-start | bytes 1572868

commit v3 on v1

--- a/solution.py
+++ b/solution.py
@@ -117,9 +117,15 @@
     table[...] = known
 
 
-def load_kernel(table, q_ref, q_out, table_out):
-    q_out[...] = q_ref[...]
-    table_out[...] = table[...]
+def load_kernel(span, group, table, q_ref, q_out):
+    in_order, _, _ = own_blocks(table)
+    for kv_head in range(q_out.shape[0]):
+        for g in range(group):
+            columns = head_columns(kv_head, g, group)
+            slots = [q_ref[slot * span : (slot + 1) * span, columns] for slot in range(2)]
+            rows = slice(g * span, (g + 1) * span)
+            q_out[kv_head, 0, rows, :] = jnp.where(in_order, slots[0], slots[1])
+            q_out[kv_head, 1, rows, :] = jnp.where(in_order, slots[1], slots[0])
 
 
 def put_block(held, block, span, rows, present):
@@ -173,26 +179,12 @@
     return slice((kv_head * group + g) * HEAD, (kv_head * group + g + 1) * HEAD)
 
 
-def query_rows(q_ref, span, kv_head, group, in_order, heads):
-    slots = [
-        jnp.concatenate(
-            [
-                q_ref[slot * span : (slot + 1) * span, head_columns(kv_head, g, group)]
-                for g in heads
-            ],
-            axis=0,
-        )
-        for slot in range(2)
-    ]
-    return jnp.where(in_order, slots[0], slots[1]), jnp.where(in_order, slots[1], slots[0])
-
-
 def attend_kernel(kv_list, span, group, q_ref, table, held, sum_ref, top_ref, total_ref):
     kv_heads = (held.shape[0] - 1) // 2
     tile = TILE_SPANS * span
     tiles = held.shape[1] // tile
     middle = tiles // 2
-    in_order, low_pos, high_pos = own_blocks(table)
+    _, low_pos, high_pos = own_blocks(table)
     gap = lax.broadcasted_iota(jnp.int32, (span, tile), 1) - lax.broadcasted_iota(
         jnp.int32, (span, tile), 0
     )
@@ -231,7 +223,8 @@
         )
 
     def score_all(kv_head, heads):
-        low_q, high_q = query_rows(q_ref, span, kv_head, group, in_order, heads)
+        rows = slice(heads[0] * span, (heads[-1] + 1) * span)
+        low_q, high_q = q_ref[kv_head, 0, rows, :], q_ref[kv_head, 1, rows, :]
         full_s = scores(high_q, keys_at(kv_head, 0, middle + 1))
         high_s = [full_s[:, t * tile : (t + 1) * tile] for t in range(middle + 1)]
         high_s[middle] = masked(high_s[middle], middle, high_pos)
@@ -304,7 +297,7 @@
     copies = []
     for kv_head, (stage, at) in enumerate(where):
         sum_ref, top_ref, total_ref = states[3 * stage : 3 * stage + 3]
-        queries = query_rows(q_ref, span, kv_head, group, in_order, range(group))
+        queries = [q_ref[kv_head, side] for side in range(2)]
         rows_k = rows_of(stage, kv_head * HEAD)
         rows_v = rows_of(stage, width + kv_head * HEAD)
         rows_v = jnp.concatenate([rows_v, jnp.ones(rows_v.shape, rows_v.dtype)], axis=1)
@@ -371,25 +364,22 @@
         [vmem],
         out_specs=vmem,
     )(span_order.reshape(1, -1))
-    q_held, loaded = call(
-        load_kernel,
-        (
-            jax.ShapeDtypeStruct(queries.shape, queries.dtype),
-            jax.ShapeDtypeStruct(table.shape, table.dtype),
-        ),
+    q_held = call(
+        functools.partial(load_kernel, span, group),
+        jax.ShapeDtypeStruct((kv_heads, 2, group * span, HEAD), queries.dtype),
         [vmem, vmem],
-        out_specs=(vmem, vmem),
+        out_specs=vmem,
     )(table, queries)
     lacks = [
         [n for n, e in enumerate(plan) if e[0] == far or (e[0] == far - 1 and not e[3])],
         [n for n, e in enumerate(plan) if e[0] == far],
     ]
-    stages = [list(range(kv_heads - 1)), list(range(kv_heads - 1, kv_heads))]
+    stages = [list(range(kv_heads // 2)), list(range(kv_heads // 2, kv_heads))]
     held_shape = jax.ShapeDtypeStruct((2 * kv_heads + 1, count, HEAD), jnp.bfloat16)
     held = None
     states = []
 
-    def place(numbers, held, source):
+    def place(numbers, held):
         kernel = (
             functools.partial(place_first, numbers, lacks[0], span)
             if held is None
@@ -399,7 +389,7 @@
         extra = {} if held is None else {"input_output_aliases": {1: 0}}
         return call(
             kernel, held_shape, [vmem] * (1 + len(before) + len(numbers)), out_specs=vmem, **extra
-        )(source, *before, *[pieces[number][0] for number in numbers])
+        )(table, *before, *[pieces[number][0] for number in numbers])
 
     def attend(stage, held):
         shape = jax.ShapeDtypeStruct((len(stages[stage]), 2, group * span, HEAD), jnp.float32)
@@ -418,10 +408,10 @@
             if ready and number not in placed:
                 numbers.append(number)
         placed.update(numbers)
-        held = place(numbers, held, loaded if step == far else table)
+        held = place(numbers, held)
     states += attend(0, held)
     rest = [number for number in lacks[0] if number not in lacks[1]]
-    held = place(rest, held, table)
+    held = place(rest, held)
     states += attend(1, held)
     numbers = lacks[0]
     return call(

time: 28.4 us -> 28.5 us (level)
  no operation moved by 1% of the time
where the time goes in v3:
time: 28.5 us; the launch traced here: 28.3 us
  starting transfers between devices  14.2 us (50%)
  waiting for transfers between devices  5.8 us (20%)
  Pallas kernels  5.57 us (20%)
  local copies, waits for them, and re-layouts  1.69 us (6%)
  other arithmetic  0.88 us (3%)
    ppermute x7, starting transfers between devices, send(): return lax.ppermute(array, 'blk', ring_pairs(size, sender, receiver, hops))  12 us
    ppermute x7, waiting for transfers between devices, send(): return lax.ppermute(array, 'blk', ring_pairs(size, sender, receiver, hops))  5.78 us
    pallas_call x2, Pallas kernels, attend(): call(functools.partial(attend_kernel, stages[stage], span, group), (shape...  2.56 us
    ppermute x8, starting transfers between devices, swap(): return lax.ppermute(array, 'blk', mate_pairs(size))  2.2 us
    pallas_call x1, Pallas kernels, attended(): call(functools.partial(finish_kernel, numbers, lacks, stages, span, group...  1.86 us
    unnamed x4, local copies, waits for them, and re-layouts  1.69 us
    max x1, other arithmetic, attended(): jnp.maximum(lax.pad(keys, lowest, ((0, 0, 0), (0, width, 0))), lax.pad(va...  0.88 us
    pallas_call x4, Pallas kernels, place(): call(kernel, held_shape, [vmem] * (1 + len(before) + len(numbers)), out_s...  0.83 us
  transfers between devices with their start and end apart: 15, of which 4 were waited for; matrix products, arithmetic and copies ran while one was open for 0% of the time, Pallas kernels for 13%

profile of v3, /device:TPU:0, one launch (start us, length us, event | category | flops | bytes accessed | tf_op | source)
XLA Modules:
  0.0 28.3 jit_solution(14657496315278952942)
XLA Ops:
  0.0 0.9 %pad_maximum_fusion.refs_0_ = bf16[64,1024]{1,0:T(8,128)(2,1)S(1)} fusion(bf16[64,512]{1,0:T(8,128)(2,1)} %param.6, bf16[64,512]{1,0:T(8,128)(2,1)} %param.5), kind=kLoop, calls=%fused_computation | loop fusion | flops 262144 | bytes 262144 | tf_op jit(solution)/shard_map/max | solution.py:354
  0.9 0.6 %collective-permute-start.4 = (bf16[64,1024]{1,0:T(8,128)(2,1)S(1)}, bf16[64,1024]{1,0:T(8,128)(2,1)S(1)}, u32[]{:S(2)}, u32[]{:S(2)}) collective-permute-start(bf16[64,1024]{1,0:T(8,128)(2,1)S(1)} %pad_maximum_fusion.refs_0_), channel_id=1, source_target_pairs={{0,1},{1,0},{2,3},{3,2},{4,5},{5,4},{6,7},{7,6},{8,9},{9,8},{10,11... | collective-permute-start | bytes 393224 | tf_op jit(solution)/shard_map/ppermute | solution.py:50
  1.4 2.7 %collective-permute-start = (bf16[64,1024]{1,0:T(8,128)(2,1)S(1)}, bf16[64,1024]{1,0:T(8,128)(2,1)S(1)}, u32[]{:S(2)}, u32[]{:S(2)}) collective-permute-start(bf16[64,1024]{1,0:T(8,128)(2,1)S(1)} %pad_maximum_fusion.refs_0_), channel_id=1, source_target_pairs={{0,5},{1,2},{2,1},{3,6},{4,9},{5,0},{6,3},{7,10},{8,13},{9,4},{10,... | collective-permute-start | bytes 393224 | tf_op jit(solution)/shard_map/ppermute | solution.py:53
  4.1 1.0 %collective-permute-start.5 = (bf16[64,1024]{1,0:T(8,128)(2,1)S(1)}, bf16[64,1024]{1,0:T(8,128)(2,1)S(1)}, u32[]{:S(2)}, u32[]{:S(2)}) collective-permute-start(bf16[64,1024]{1,0:T(8,128)(2,1)S(1)} %collective-permute-done.4.refs_1_), channel_id=1, source_target_pairs={{0,5},{1,2},{2,1},{3,6},{4,9},{5,0},{6,3},{7,10},{8,13},{9,4},{10,... | collective-permute-start | bytes 393224 | tf_op jit(solution)/shard_map/ppermute | solution.py:53
  5.1 1.7 %collective-permute-done.refs_2_ = bf16[64,1024]{1,0:T(8,128)(2,1)S(1)} collective-permute-done((bf16[64,1024]{1,0:T(8,128)(2,1)S(1)}, bf16[64,1024]{1,0:T(8,128)(2,1)S(1)}, u32[]{:S(2)}, u32[]{:S(2)}) %collective-permute-start) | collective-permute-done | bytes 131104 | tf_op jit(solution)/shard_map/ppermute | solution.py:53
  6.8 2.0 %collective-permute-start.1 = (bf16[64,1024]{1,0:T(8,128)(2,1)S(1)}, bf16[64,1024]{1,0:T(8,128)(2,1)S(1)}, u32[]{:S(2)}, u32[]{:S(2)}) collective-permute-start(bf16[64,1024]{1,0:T(8,128)(2,1)S(1)} %collective-permute-done.refs_2_), channel_id=1, source_target_pairs={{0,3},{1,4},{2,7},{3,0},{4,1},{5,8},{6,11},{7,2},{8,5},{9,12},{10,... | collective-permute-start | bytes 393224 | tf_op jit(solution)/shard_map/ppermute | solution.py:53
  8.8 1.1 %collective-permute-start.6 = (bf16[64,1024]{1,0:T(8,128)(2,1)S(1)}, bf16[64,1024]{1,0:T(8,128)(2,1)S(1)}, u32[]{:S(2)}, u32[]{:S(2)}) collective-permute-start(bf16[64,1024]{1,0:T(8,128)(2,1)S(1)} %collective-permute-done.5.refs_3_), channel_id=1, source_target_pairs={{0,3},{1,4},{2,7},{3,0},{4,1},{5,8},{6,11},{7,2},{8,5},{9,12},{10,... | collective-permute-start | bytes 393224 | tf_op jit(solution)/shard_map/ppermute | solution.py:53
  9.9 1.5 %collective-permute-done.1.refs_2_ = bf16[64,1024]{1,0:T(8,128)(2,1)S(1)} collective-permute-done((bf16[64,1024]{1,0:T(8,128)(2,1)S(1)}, bf16[64,1024]{1,0:T(8,128)(2,1)S(1)}, u32[]{:S(2)}, u32[]{:S(2)}) %collective-permute-start.1) | collective-permute-done | bytes 131104 | tf_op jit(solution)/shard_map/ppermute | solution.py:53
  11.4 2.1 %collective-permute-start.2 = (bf16[64,1024]{1,0:T(8,128)(2,1)S(1)}, bf16[64,1024]{1,0:T(8,128)(2,1)S(1)}, u32[]{:S(2)}, u32[]{:S(2)}) collective-permute-start(bf16[64,1024]{1,0:T(8,128)(2,1)S(1)} %collective-permute-done.1.refs_2_), channel_id=1, source_target_pairs={{0,5},{1,2},{2,1},{3,6},{4,9},{5,0},{6,3},{7,10},{8,13},{9,4},{10,... | collective-permute-start | bytes 393224 | tf_op jit(solution)/shard_map/ppermute | solution.py:53
  13.5 0.5 %collective-permute-start.12 = (bf16[64,1024]{1,0:T(8,128)(2,1)S(1)}, bf16[64,1024]{1,0:T(8,128)(2,1)S(1)}, u32[]{:S(2)}, u32[]{:S(2)}) collective-permute-start(bf16[64,1024]{1,0:T(8,128)(2,1)S(1)} %collective-permute-done.5.refs_3_), channel_id=1, source_target_pairs={{0,1},{1,0},{2,3},{3,2},{4,5},{5,4},{6,7},{7,6},{8,9},{9,8},{10,11... | collective-permute-start | bytes 393224 | tf_op jit(solution)/shard_map/ppermute | solution.py:50
  14.0 1.2 %collective-permute-start.7 = (bf16[64,1024]{1,0:T(8,128)(2,1)S(1)}, bf16[64,1024]{1,0:T(8,128)(2,1)S(1)}, u32[]{:S(2)}, u32[]{:S(2)}) collective-permute-start(bf16[64,1024]{1,0:T(8,128)(2,1)S(1)} %collective-permute-done.6.refs_3_), channel_id=1, source_target_pairs={{0,5},{1,2},{2,1},{3,6},{4,9},{5,0},{6,3},{7,10},{8,13},{9,4},{10,... | collective-permute-start | bytes 393224 | tf_op jit(solution)/shard_map/ppermute | solution.py:53
  15.2 1.0 %collective-permute-done.2.refs_2_ = bf16[64,1024]{1,0:T(8,128)(2,1)S(1)} collective-permute-done((bf16[64,1024]{1,0:T(8,128)(2,1)S(1)}, bf16[64,1024]{1,0:T(8,128)(2,1)S(1)}, u32[]{:S(2)}, u32[]{:S(2)}) %collective-permute-start.2) | collective-permute-done | bytes 131104 | tf_op jit(solution)/shard_map/ppermute | solution.py:53
  16.1 2.0 %collective-permute-start.9 = (bf16[64,1024]{1,0:T(8,128)(2,1)S(1)}, bf16[64,1024]{1,0:T(8,128)(2,1)S(1)}, u32[]{:S(2)}, u32[]{:S(2)}) collective-permute-start(bf16[64,1024]{1,0:T(8,128)(2,1)S(1)} %collective-permute-done.2.refs_2_), channel_id=1, source_target_pairs={{0,3},{1,4},{2,7},{3,0},{4,1},{5,8},{6,11},{7,2},{8,5},{9,12},{10,... | collective-permute-start | bytes 393224 | tf_op jit(solution)/shard_map/ppermute | solution.py:53
  18.1 0.5 %collective-permute-start.14 = (bf16[64,1024]{1,0:T(8,128)(2,1)S(1)}, bf16[64,1024]{1,0:T(8,128)(2,1)S(1)}, u32[]{:S(2)}, u32[]{:S(2)}) collective-permute-start(bf16[64,1024]{1,0:T(8,128)(2,1)S(1)} %collective-permute-done.6.refs_3_), channel_id=1, source_target_pairs={{0,1},{1,0},{2,3},{3,2},{4,5},{5,4},{6,7},{7,6},{8,9},{9,8},{10,11... | collective-permute-start | bytes 393224 | tf_op jit(solution)/shard_map/ppermute | solution.py:50
  18.7 0.4 %collective-permute-start.8 = (bf16[64,1024]{1,0:T(8,128)(2,1)S(1)}, bf16[64,1024]{1,0:T(8,128)(2,1)S(1)}, u32[]{:S(2)}, u32[]{:S(2)}) collective-permute-start(bf16[64,1024]{1,0:T(8,128)(2,1)S(1)} %collective-permute-done.7.refs_3_), channel_id=1, source_target_pairs={{0,1},{1,0},{2,3},{3,2},{4,5},{5,4},{6,7},{7,6},{8,9},{9,8},{10,11... | collective-permute-start | bytes 393224 | tf_op jit(solution)/shard_map/ppermute | solution.py:50
  19.2 1.6 %collective-permute-done.9.refs_2_ = bf16[64,1024]{1,0:T(8,128)(2,1)S(1)} collective-permute-done((bf16[64,1024]{1,0:T(8,128)(2,1)S(1)}, bf16[64,1024]{1,0:T(8,128)(2,1)S(1)}, u32[]{:S(2)}, u32[]{:S(2)}) %collective-permute-start.9) | collective-permute-done | bytes 131104 | tf_op jit(solution)/shard_map/ppermute | solution.py:53
  20.9 0.7 %copy-done.1 = s32[32]{0:T(128)S(1)} copy-done((s32[32]{0:T(128)S(1)}, s32[32]{0:T(128)}, u32[]{:S(2)}) %copy-start.1) | copy-done | bytes 152
  21.7 1.0 %copy-done = bf16[64,4096]{1,0:T(8,128)(2,1)S(1)} copy-done((bf16[64,4096]{1,0:T(8,128)(2,1)S(1)}, bf16[64,4096]{1,0:T(8,128)(2,1)}, u32[]{:S(2)}) %copy-start) | copy-done | bytes 524312
  22.9 0.3 shard_map.48.held_in
  23.2 0.2 shard_map.49.held_in
  23.4 0.2 shard_map.50.held.held_in
  23.7 1.3 %shard_map.51 = (f32[2,2,256,128]{3,2,1,0:T(8,128)S(1)}, f32[2,2,256,128]{3,2,1,0:T(8,128)S(1)}, f32[2,2,256,128]{3,2,1,0:T(8,128)S(1)}) custom-call(bf16[4,2,256,128]{3,2,1,0:T(8,128)(2,1)S(1)} %shard_map.47.q_ref, s32[1,128]{1,0:T(1,128)S(1)} %shard_map.46.table, bf16[9,1024,128]{2,1,0:T(8,128)(2,1)S(1)} %shard_map.50.held.held_in), custom_call_target="tpu_custom_call" | custom-call | tf_op jit(solution)/shard_map/pallas_call | solution.py:396
  25.1 1.3 %shard_map.53 = (f32[2,2,256,128]{3,2,1,0:T(8,128)S(1)}, f32[2,2,256,128]{3,2,1,0:T(8,128)S(1)}, f32[2,2,256,128]{3,2,1,0:T(8,128)S(1)}) custom-call(bf16[4,2,256,128]{3,2,1,0:T(8,128)(2,1)S(1)} %shard_map.47.q_ref, s32[1,128]{1,0:T(1,128)S(1)} %shard_map.46.table, bf16[9,1024,128]{2,1,0:T(8,128)(2,1)S(1)} %shard_map.52.held), custom_call_target="tpu_custom_call" | custom-call | tf_op jit(solution)/shard_map/pallas_call | solution.py:396
  26.4 1.9 %shard_map.54 = bf16[64,4096]{1,0:T(8,128)(2,1)} custom-call(bf16[4,2,256,128]{3,2,1,0:T(8,128)(2,1)S(1)} %shard_map.47.q_ref, s32[1,128]{1,0:T(1,128)S(1)} %shard_map.46.table, bf16[64,1024]{1,0:T(8,128)(2,1)S(1)} %collective-permute-done.3.refs_0_, bf16[64,1024]{1,0:T(8,128)(2,1)S(1)} %collective-permute-done.8.refs_1_, ...), custom_call_target="tpu_custom_call" | custom-call | tf_op jit(solution)/shard_map/pallas_call | solution.py:417
  (20 shorter events, 0.7 us)
Async XLA Ops:
  0.9 3.2 %collective-permute-start.4 = (bf16[64,1024]{1,0:T(8,128)(2,1)S(1)}, bf16[64,1024]{1,0:T(8,128)(2,1)S(1)}, u32[]{:S(2)}, u32[]{:S(2)}) collective-permute-start(bf16[64,1024]{1,0:T(8,128)(2,1)S(1)} %pad_maximum_fusion.refs_0_), channel_id=1, source_target_pairs={{0,1},{1,0},{2,3},{3,2},{4,5},{5,4},{6,7},{7,6},{8,9},{9,8},{10,11... | collective-permute-start | bytes 393224 | tf_op jit(solution)/shard_map/ppermute | solution.py:50
  1.4 5.3 %collective-permute-start = (bf16[64,1024]{1,0:T(8,128)(2,1)S(1)}, bf16[64,1024]{1,0:T(8,128)(2,1)S(1)}, u32[]{:S(2)}, u32[]{:S(2)}) collective-permute-start(bf16[64,1024]{1,0:T(8,128)(2,1)S(1)} %pad_maximum_fusion.refs_0_), channel_id=1, source_target_pairs={{0,5},{1,2},{2,1},{3,6},{4,9},{5,0},{6,3},{7,10},{8,13},{9,4},{10,... | collective-permute-start | bytes 393224 | tf_op jit(solution)/shard_map/ppermute | solution.py:53
  4.1 4.6 %collective-permute-start.5 = (bf16[64,1024]{1,0:T(8,128)(2,1)S(1)}, bf16[64,1024]{1,0:T(8,128)(2,1)S(1)}, u32[]{:S(2)}, u32[]{:S(2)}) collective-permute-start(bf16[64,1024]{1,0:T(8,128)(2,1)S(1)} %collective-permute-done.4.refs_1_), channel_id=1, source_target_pairs={{0,5},{1,2},{2,1},{3,6},{4,9},{5,0},{6,3},{7,10},{8,13},{9,4},{10,... | collective-permute-start | bytes 393224 | tf_op jit(solution)/shard_map/ppermute | solution.py:53
  6.8 4.6 %collective-permute-start.1 = (bf16[64,1024]{1,0:T(8,128)(2,1)S(1)}, bf16[64,1024]{1,0:T(8,128)(2,1)S(1)}, u32[]{:S(2)}, u32[]{:S(2)}) collective-permute-start(bf16[64,1024]{1,0:T(8,128)(2,1)S(1)} %collective-permute-done.refs_2_), channel_id=1, source_target_pairs={{0,3},{1,4},{2,7},{3,0},{4,1},{5,8},{6,11},{7,2},{8,5},{9,12},{10,... | collective-permute-start | bytes 393224 | tf_op jit(solution)/shard_map/ppermute | solution.py:53
  8.8 5.3 %collective-permute-start.6 = (bf16[64,1024]{1,0:T(8,128)(2,1)S(1)}, bf16[64,1024]{1,0:T(8,128)(2,1)S(1)}, u32[]{:S(2)}, u32[]{:S(2)}) collective-permute-start(bf16[64,1024]{1,0:T(8,128)(2,1)S(1)} %collective-permute-done.5.refs_3_), channel_id=1, source_target_pairs={{0,3},{1,4},{2,7},{3,0},{4,1},{5,8},{6,11},{7,2},{8,5},{9,12},{10,... | collective-permute-start | bytes 393224 | tf_op jit(solution)/shard_map/ppermute | solution.py:53
  11.4 4.7 %collective-permute-start.2 = (bf16[64,1024]{1,0:T(8,128)(2,1)S(1)}, bf16[64,1024]{1,0:T(8,128)(2,1)S(1)}, u32[]{:S(2)}, u32[]{:S(2)}) collective-permute-start(bf16[64,1024]{1,0:T(8,128)(2,1)S(1)} %collective-permute-done.1.refs_2_), channel_id=1, source_target_pairs={{0,5},{1,2},{2,1},{3,6},{4,9},{5,0},{6,3},{7,10},{8,13},{9,4},{10,... | collective-permute-start | bytes 393224 | tf_op jit(solution)/shard_map/ppermute | solution.py:53
  13.5 4.6 %collective-permute-start.11 = (bf16[64,1024]{1,0:T(8,128)(2,1)S(1)}, bf16[64,1024]{1,0:T(8,128)(2,1)S(1)}, u32[]{:S(2)}, u32[]{:S(2)}) collective-permute-start(bf16[64,1024]{1,0:T(8,128)(2,1)S(1)} %collective-permute-done.refs_2_), channel_id=1, source_target_pairs={{0,1},{1,0},{2,3},{3,2},{4,5},{5,4},{6,7},{7,6},{8,9},{9,8},{10,11... | collective-permute-start | bytes 393224 | tf_op jit(solution)/shard_map/ppermute | solution.py:50
  13.5 5.1 %collective-permute-start.12 = (bf16[64,1024]{1,0:T(8,128)(2,1)S(1)}, bf16[64,1024]{1,0:T(8,128)(2,1)S(1)}, u32[]{:S(2)}, u32[]{:S(2)}) collective-permute-start(bf16[64,1024]{1,0:T(8,128)(2,1)S(1)} %collective-permute-done.5.refs_3_), channel_id=1, source_target_pairs={{0,1},{1,0},{2,3},{3,2},{4,5},{5,4},{6,7},{7,6},{8,9},{9,8},{10,11... | collective-permute-start | bytes 393224 | tf_op jit(solution)/shard_map/ppermute | solution.py:50
  14.0 4.7 %collective-permute-start.7 = (bf16[64,1024]{1,0:T(8,128)(2,1)S(1)}, bf16[64,1024]{1,0:T(8,128)(2,1)S(1)}, u32[]{:S(2)}, u32[]{:S(2)}) collective-permute-start(bf16[64,1024]{1,0:T(8,128)(2,1)S(1)} %collective-permute-done.6.refs_3_), channel_id=1, source_target_pairs={{0,5},{1,2},{2,1},{3,6},{4,9},{5,0},{6,3},{7,10},{8,13},{9,4},{10,... | collective-permute-start | bytes 393224 | tf_op jit(solution)/shard_map/ppermute | solution.py:53
  16.1 4.6 %collective-permute-start.9 = (bf16[64,1024]{1,0:T(8,128)(2,1)S(1)}, bf16[64,1024]{1,0:T(8,128)(2,1)S(1)}, u32[]{:S(2)}, u32[]{:S(2)}) collective-permute-start(bf16[64,1024]{1,0:T(8,128)(2,1)S(1)} %collective-permute-done.2.refs_2_), channel_id=1, source_target_pairs={{0,3},{1,4},{2,7},{3,0},{4,1},{5,8},{6,11},{7,2},{8,5},{9,12},{10,... | collective-permute-start | bytes 393224 | tf_op jit(solution)/shard_map/ppermute | solution.py:53
  18.1 5.3 %collective-permute-start.13 = (bf16[64,1024]{1,0:T(8,128)(2,1)S(1)}, bf16[64,1024]{1,0:T(8,128)(2,1)S(1)}, u32[]{:S(2)}, u32[]{:S(2)}) collective-permute-start(bf16[64,1024]{1,0:T(8,128)(2,1)S(1)} %collective-permute-done.1.refs_2_), channel_id=1, source_target_pairs={{0,1},{1,0},{2,3},{3,2},{4,5},{5,4},{6,7},{7,6},{8,9},{9,8},{10,11... | collective-permute-start | bytes 393224 | tf_op jit(solution)/shard_map/ppermute | solution.py:50
  18.1 5.3 %collective-permute-start.14 = (bf16[64,1024]{1,0:T(8,128)(2,1)S(1)}, bf16[64,1024]{1,0:T(8,128)(2,1)S(1)}, u32[]{:S(2)}, u32[]{:S(2)}) collective-permute-start(bf16[64,1024]{1,0:T(8,128)(2,1)S(1)} %collective-permute-done.6.refs_3_), channel_id=1, source_target_pairs={{0,1},{1,0},{2,3},{3,2},{4,5},{5,4},{6,7},{7,6},{8,9},{9,8},{10,11... | collective-permute-start | bytes 393224 | tf_op jit(solution)/shard_map/ppermute | solution.py:50
  18.6 6.3 %collective-permute-start.3 = (bf16[64,1024]{1,0:T(8,128)(2,1)S(1)}, bf16[64,1024]{1,0:T(8,128)(2,1)S(1)}, u32[]{:S(2)}, u32[]{:S(2)}) collective-permute-start(bf16[64,1024]{1,0:T(8,128)(2,1)S(1)} %collective-permute-done.2.refs_2_), channel_id=1, source_target_pairs={{0,1},{1,0},{2,3},{3,2},{4,5},{5,4},{6,7},{7,6},{8,9},{9,8},{10,11... | collective-permute-start | bytes 393224 | tf_op jit(solution)/shard_map/ppermute | solution.py:50
  18.7 6.2 %collective-permute-start.8 = (bf16[64,1024]{1,0:T(8,128)(2,1)S(1)}, bf16[64,1024]{1,0:T(8,128)(2,1)S(1)}, u32[]{:S(2)}, u32[]{:S(2)}) collective-permute-start(bf16[64,1024]{1,0:T(8,128)(2,1)S(1)} %collective-permute-done.7.refs_3_), channel_id=1, source_target_pairs={{0,1},{1,0},{2,3},{3,2},{4,5},{5,4},{6,7},{7,6},{8,9},{9,8},{10,11... | collective-permute-start | bytes 393224 | tf_op jit(solution)/shard_map/ppermute | solution.py:50
  20.8 5.6 %collective-permute-start.10 = (bf16[64,1024]{1,0:T(8,128)(2,1)S(1)}, bf16[64,1024]{1,0:T(8,128)(2,1)S(1)}, u32[]{:S(2)}, u32[]{:S(2)}) collective-permute-start(bf16[64,1024]{1,0:T(8,128)(2,1)S(1)} %collective-permute-done.9.refs_2_), channel_id=1, source_target_pairs={{0,1},{1,0},{2,3},{3,2},{4,5},{5,4},{6,7},{7,6},{8,9},{9,8},{10,11... | collective-permute-start | bytes 393224 | tf_op jit(solution)/shard_map/ppermute | solution.py:50
  20.9 0.7 %copy-start.1 = (s32[32]{0:T(128)S(1)}, s32[32]{0:T(128)}, u32[]{:S(2)}) copy-start(s32[32]{0:T(128)} %param.7) | copy-start | bytes 388
  21.7 1.0 %copy-start = (bf16[64,4096]{1,0:T(8,128)(2,1)S(1)}, bf16[64,4096]{1,0:T(8,128)(2,1)}, u32[]{:S(2)}) copy-start(bf16[64,4096]{1,0:T(8,128)(2,1)} %q_ref.1) | copy-start | bytes 1572868
